TPU v7x, 128 devices: a whole 4x4x4 slice. The times are simulated.
128 devices in a mesh: row: 2 (over core), dep: 64 (over z, y, x).
Axes of the slice: x: 4, y: 4, z: 4, core: 2. Of those that a mesh axis runs over, the one named last changes fastest.
Arguments:
- x_vol: bfloat16 [2, 128, 8, 256, 128], P(None, 'dep', 'row')
- w_conv1: bfloat16 [3, 3, 3, 128, 128], replicated
- w_conv2: bfloat16 [3, 3, 3, 128, 128], replicated
- g_out: bfloat16 [2, 128, 8, 256, 128], P(None, 'dep', 'row')
Outputs:
- output 1: bfloat16 [2, 128, 8, 256, 128], P(None, 'dep', 'row')
- output 2: bfloat16 [2, 128, 8, 256, 128], P(None, 'dep', 'row')
- output 3: float32 [3, 3, 3, 128, 128], replicated
- output 4: float32 [3, 3, 3, 128, 128], replicated
All inputs are finite; a program needn't handle non-finite values.
Results may differ from a plain program's by a relative error of at most 0.00930195.
Values are sent between devices in bfloat16 or wider.
A program may use at most 1 GiB of HBM per device.

v0:
```python
import functools
import math

import jax
import jax.numpy as jnp
from jax import lax
from jax.experimental import pallas as pl
from jax.experimental.pallas import tpu as pltpu
from jax.sharding import PartitionSpec as P

MESH = pl.DeviceIdType.MESH
F32 = jnp.float32
BF16 = jnp.bfloat16
S2PI = math.sqrt(2.0 / math.pi)
C3 = 0.044715

NB, ND, NH, NC = 2, 2, 4, 128
RING = 4
TAPS = 28
TQ = TAPS // RING


def kernel(width, depth_count,
           x_hbm, w1_hbm, w2_hbm, g_hbm,
           y_hbm, dx_hbm, dw1_hbm, dw2_hbm,
           xe, ge, ze, ae, w1, w2, acc1, acc2, dgel, zt, at, obuf,
           p2, p1, cr, r1, bz, r2, xb, ds, es,
           hs_send, hs_recv, rs_send, rs_recv, ar_send, ar_recv, lsem, osem):
    rows = NH * width
    row = lax.axis_index("row")
    dep = lax.axis_index("dep")
    x = lax.rem(dep, RING)
    y = lax.rem(dep // RING, RING)
    z = dep // (RING * RING)
    other = 1 - row
    exts = (xe, ge, ze, ae)
    edge = (NH - 1) - (NH - 1) * row
    my_pad = (NH + 1) * row

    def ring_dep(axis, off):
        if axis == "x":
            return dep - x + lax.rem(x + off, RING)
        if axis == "y":
            return dep - RING * y + RING * lax.rem(y + off, RING)
        return dep - RING * RING * z + RING * RING * lax.rem(z + off, RING)

    def rdma(src, dst, ssem, rsem, dev):
        return pltpu.make_async_remote_copy(src_ref=src, dst_ref=dst, send_sem=ssem, recv_sem=rsem, device_id=dev, device_id_type=MESH)

    has_below = dep > 0
    has_above = dep < depth_count - 1

    def face(k, src_of, up, part):
        h0, hn = (edge, 1) if part == 0 else (row, NH - 1)
        d_src, d_dst = (ND - 1, 0) if up else (0, ND + 1)
        dev = (row, dep + 1) if up else (row, dep - 1)
        n = 2 * part + (0 if up else 1)
        return rdma(src_of(d_src, h0, hn), exts[k].at[:, d_dst, pl.ds(1 + h0, hn)], hs_send.at[k, n], hs_recv.at[k, n], dev)

    def side(k, src_of):
        return rdma(src_of(None, edge, 1), exts[k].at[:, pl.ds(1, ND), pl.ds(my_pad, 1)], rs_send.at[k, 0], rs_recv.at[k, 0], (other, dep))

    def corner(k, up):
        d_dst = 0 if up else ND + 1
        n = 1 if up else 2
        return rdma(exts[k].at[:, d_dst, pl.ds(1 + edge, 1)], exts[k].at[:, d_dst, pl.ds(my_pad, 1)], rs_send.at[k, n], rs_recv.at[k, n], (other, dep))

    def from_hbm(ref):
        def src(d, h0, hn):
            return ref.at[:, pl.ds(0, ND) if d is None else d, pl.ds(h0, hn)]
        return src

    def from_ext(ref):
        def src(d, h0, hn):
            return ref.at[:, pl.ds(1, ND) if d is None else 1 + d, pl.ds(1 + h0, hn)]
        return src

    sources = (from_hbm(x_hbm), from_hbm(g_hbm), from_ext(ze), from_ext(ae))

    def send_faces(k):
        side(k, sources[k]).start()
        for part in range(2):
            @pl.when(has_above)
            def _():
                face(k, sources[k], True, part).start()

            @pl.when(has_below)
            def _():
                face(k, sources[k], False, part).start()

    def pass_corners(k):
        @pl.when(has_below)
        def _():
            face(k, sources[k], True, 0).wait_recv()
            corner(k, True).start()

        @pl.when(has_above)
        def _():
            face(k, sources[k], False, 0).wait_recv()
            corner(k, False).start()

    def take_faces(k):
        @pl.when(has_below)
        def _():
            face(k, sources[k], True, 1).wait_recv()
            corner(k, True).wait_recv()

        @pl.when(has_above)
        def _():
            face(k, sources[k], False, 1).wait_recv()
            corner(k, False).wait_recv()

    def finish_halo(k):
        side(k, sources[k]).wait_send()
        for part in range(2):
            @pl.when(has_above)
            def _():
                face(k, sources[k], True, part).wait_send()

            @pl.when(has_below)
            def _():
                face(k, sources[k], False, part).wait_send()

        @pl.when(has_below)
        def _():
            corner(k, True).wait_send()

        @pl.when(has_above)
        def _():
            corner(k, False).wait_send()

    barrier = pltpu.get_barrier_semaphore()
    pl.semaphore_signal(barrier, inc=1, device_id=(other, dep), device_id_type=MESH)
    for axis in ("x", "y", "z"):
        for off in range(1, RING):
            pl.semaphore_signal(barrier, inc=1, device_id=(row, ring_dep(axis, off)), device_id_type=MESH)

    for step in (1, depth_count - 1):
        pl.semaphore_signal(barrier, inc=1, device_id=(row, lax.rem(dep + step, depth_count)), device_id_type=MESH)

    loads = [
        pltpu.make_async_copy(x_hbm, xe.at[:, pl.ds(1, ND), pl.ds(1, NH)], lsem.at[0]),
        pltpu.make_async_copy(w1_hbm, w1, lsem.at[1]),
        pltpu.make_async_copy(g_hbm, ge.at[:, pl.ds(1, ND), pl.ds(1, NH)], lsem.at[2]),
        pltpu.make_async_copy(w2_hbm, w2, lsem.at[3]),
    ]
    for load in loads:
        load.start()

    pl.semaphore_wait(barrier, 12)

    send_faces(0)
    send_faces(1)

    zero_row = jnp.zeros((NB, 1, width, NC), BF16)
    for ext in exts:
        for dd in range(ND + 2):
            ext[:, dd, pl.ds(my_pad, 1)] = zero_row
    zero_face = jnp.zeros((NH + 2, width, NC), BF16)

    @pl.when(dep == 0)
    def _():
        for ext in exts:
            for b in range(NB):
                ext[b, 0] = zero_face

    @pl.when(dep == depth_count - 1)
    def _():
        for ext in exts:
            for b in range(NB):
                ext[b, ND + 1] = zero_face

    p2[TAPS - 1] = jnp.zeros((NC, NC), F32)
    p1[TAPS - 1] = jnp.zeros((NC, NC), F32)

    def lines(ext, b, dd, h0):
        return ext[b, dd, pl.ds(h0, NH)].reshape(rows, NC)

    def tap_block(w, td, th, tw, flip):
        return w[2 - td, 2 - th, 2 - tw] if flip else w[td, th, tw]

    def weights(w, cells, flip):
        zero = jnp.zeros((NC, NC), BF16)
        blocks = [[zero if t is None else tap_block(w, *t, flip) for t in line] for line in cells]
        if flip:
            return jnp.concatenate([jnp.concatenate([blocks[k][n] for k in range(len(blocks))], axis=1) for n in range(len(blocks[0]))], axis=0)
        return jnp.concatenate([jnp.concatenate(line, axis=1) for line in blocks], axis=0)

    def mul(lhs, rhs, flip):
        return lax.dot_general(lhs, rhs, (((1,), (1 if flip else 0,)), ((), ())), preferred_element_type=F32)

    def conv_inner(ext, w, acc, flip):
        cells = []
        for dd in (1, 2):
            for th in range(3):
                cells.append([(dd, th, 0), (dd, th, 1), (dd - 1, th, 0), (dd - 1, th, 1), (dd, th, 2), (dd - 1, th, 2)])
        order = ((0, 0), (0, 1), (1, 0), (1, 1), (0, 2), (1, 2))

        def one(b, carry):
            lhs = jnp.concatenate([lines(ext, b, dd, th) for dd in (1, 2) for th in range(3)], axis=1)
            for n in range(3):
                out = mul(lhs, weights(w, [line[2 * n:2 * n + 2] for line in cells], flip), flip)
                for j in range(2):
                    d, tw = order[2 * n + j]
                    acc[b, d * 3 + tw] = out[:, j * NC:(j + 1) * NC]
            return carry

        lax.fori_loop(0, NB, one, 0)

    def conv_outer(ext, w, acc, flip):
        def one(i, carry):
            b, d = i // ND, lax.rem(i, ND)
            td = 2 * d
            lhs = jnp.concatenate([lines(ext, b, 3 * d, th) for th in range(3)], axis=1)
            out = mul(lhs, weights(w, [[(td, th, tw) for tw in range(3)] for th in range(3)], flip), flip)
            for tw in range(3):
                acc[b, d * 3 + tw] += out[:, tw * NC:(tw + 1) * NC]
            return carry

        lax.fori_loop(0, NB * ND, one, 0)

    wpos = lax.broadcasted_iota(jnp.int32, (width, NC), 0)

    def from_left(v):
        return jnp.where(wpos > 0, pltpu.roll(v, 1, 0), 0.0)

    def from_right(v):
        return jnp.where(wpos < width - 1, pltpu.roll(v, width - 1, 0), 0.0)

    def each_row(acc, use):
        def one(i, carry):
            b, d, h = i // (ND * NH), lax.rem(i // NH, ND), lax.rem(i, NH)
            at_rows = pl.ds(pl.multiple_of(h * width, width), width)
            total = acc[b, d * 3 + 1, at_rows] + from_left(acc[b, d * 3, at_rows]) + from_right(acc[b, d * 3 + 2, at_rows])
            use(i, b, d, h, total)
            return carry

        lax.fori_loop(0, NB * ND * NH, one, 0)

    def after_conv1(i, b, d, h, total):
        a = total.astype(BF16).astype(F32)
        a2 = a * a
        t = jnp.tanh(S2PI * (a + C3 * (a2 * a)))
        cdf = 0.5 * (1.0 + t)
        gel = a * cdf
        dgel[i] = cdf + (0.5 * a * ((1.0 + t) * (1.0 - t))) * (S2PI * (1.0 + 3.0 * C3 * a2))
        ze[b, 1 + d, 1 + h] = gel.astype(BF16)
        for tw, v in enumerate((from_left(gel), gel, from_right(gel))):
            zt[i, pl.ds(tw * NC, NC)] = v.astype(BF16).T

    def after_conv_g(i, b, d, h, total):
        da = total * dgel[i]
        ae[b, 1 + d, 1 + h] = da.astype(BF16)
        for tw, v in enumerate((from_right(da), da, from_left(da))):
            at[i, pl.ds(tw * NC, NC)] = v.astype(BF16).T

    def after_add(ext):
        def use(i, b, d, h, total):
            obuf[b, d, h] = (total + ext[b, 1 + d, 1 + h].astype(F32)).astype(BF16)
        return use

    def weight_grad(own_t, ext, part, swap):
        def rhs(td, th):
            d0, h0 = (2 - td, 2 - th) if swap else (td, th)
            return jnp.concatenate([lines(ext, b, d + d0, h0) for b in range(NB) for d in range(ND)], axis=0)

        def product(right):
            lhs = jnp.concatenate([own_t[i] for i in range(NB * ND * NH)], axis=1)
            return jnp.dot(lhs, right, preferred_element_type=F32)

        def put(out, n, td, th):
            for tw in range(3):
                blk = out[tw * NC:(tw + 1) * NC, n * NC:(n + 1) * NC]
                part[td * 9 + th * 3 + tw] = blk if swap else blk.T

        def one(td, carry):
            out = product(jnp.concatenate([rhs(td, 0), rhs(td, 1)], axis=1))
            put(out, 0, td, 0)
            put(out, 1, td, 1)
            return carry

        lax.fori_loop(0, 3, one, 0)
        out = product(jnp.concatenate([rhs(0, 2), rhs(1, 2)], axis=1))
        put(out, 0, 0, 2)
        put(out, 1, 1, 2)
        put(product(rhs(2, 2)), 0, 2, 2)

    half, quarter = NC // 2, NC // 8
    axes = (("y", "z"), ("z", "y"))
    coord = {"x": x, "y": y, "z": z}
    parts = (p2, p1)
    outs = (dw2_hbm, dw1_hbm)

    def sems(s, n):
        return ar_send.at[s, n], ar_recv.at[s, n]

    def pair_copy(s):
        theirs = pl.ds(pl.multiple_of(other * half, half), half)
        return rdma(parts[s].at[:, theirs], cr.at[s], *sems(s, 0), (other, dep))

    def first_copy(s, off):
        axis = axes[s][0]
        j = lax.rem(coord[axis] + off, RING)
        src = parts[s].at[:, pl.ds(pl.multiple_of(row * half + j * quarter, quarter), quarter)]
        return rdma(src, r1.at[s, off - 1], *sems(s, off), (row, ring_dep(axis, off)))

    def second_copy(s, off):
        axis = axes[s][1]
        j = lax.rem(coord[axis] + off, RING)
        return rdma(bz.at[s, pl.ds(j * TQ, TQ)], r2.at[s, off - 1], *sems(s, 3 + off), (row, ring_dep(axis, off)))

    def third_copy(s, off, slot):
        return rdma(xb.at[s, slot], xb.at[s, slot], *sems(s, 6 + off), (row, ring_dep("x", off)))

    def fourth_copy(s, off, j):
        axis = axes[s][1]
        return rdma(ds.at[s, pl.ds(j * TQ, TQ)], ds.at[s, pl.ds(j * TQ, TQ)], *sems(s, 9 + off), (row, ring_dep(axis, off)))

    def fifth_copy(s, off, j):
        axis = axes[s][0]
        return rdma(ds.at[s], es.at[s, :, pl.ds(pl.multiple_of(j * quarter, quarter), quarter)], *sems(s, 12 + off), (row, ring_dep(axis, off)))

    my_half = pl.ds(pl.multiple_of(row * half, half), half)

    def last_copy(s):
        return rdma(es.at[s, pl.ds(0, 27)], outs[s].at[:, my_half], *sems(s, 16), (other, dep))

    def own_copy(s):
        return pltpu.make_async_copy(es.at[s, pl.ds(0, 27)], outs[s].at[:, my_half], osem.at[2 + s])

    def step_pair(s):
        pair_copy(s).wait_recv()

        def add(t, carry):
            parts[s][t, my_half] += cr[s, t]
            return carry

        lax.fori_loop(0, TAPS, add, 0)
        for off in (2, 1, 3):
            first_copy(s, off).start()

    def step_first(s):
        for off in (1, 2, 3):
            first_copy(s, off).wait_recv()
        mine = pl.ds(pl.multiple_of(row * half + coord[axes[s][0]] * quarter, quarter), quarter)

        def add(t, carry):
            bz[s, t] = (parts[s][t, mine] + r1[s, 0, t]) + (r1[s, 1, t] + r1[s, 2, t])
            return carry

        lax.fori_loop(0, TAPS, add, 0)
        for off in (2, 1, 3):
            second_copy(s, off).start()

    def step_second(s):
        for off in (1, 2, 3):
            second_copy(s, off).wait_recv()
        c = coord[axes[s][1]]

        def add(t, carry):
            xb[s, x, t] = (bz[s, c * TQ + t] + r2[s, 0, t]) + (r2[s, 1, t] + r2[s, 2, t])
            return carry

        lax.fori_loop(0, TQ, add, 0)
        for off in (2, 1, 3):
            third_copy(s, off, x).start()

    def step_third(s):
        for off in (1, 2, 3):
            third_copy(s, off, lax.rem(x + RING - off, RING)).wait_recv()
        c = coord[axes[s][1]]

        def add(t, carry):
            ds[s, c * TQ + t] = (xb[s, 0, t] + xb[s, 1, t]) + (xb[s, 2, t] + xb[s, 3, t])
            return carry

        lax.fori_loop(0, TQ, add, 0)
        for off in (2, 1, 3):
            fourth_copy(s, off, c).start()

    def step_fourth(s):
        c = coord[axes[s][1]]
        for off in (1, 2, 3):
            fourth_copy(s, off, lax.rem(c + RING - off, RING)).wait_recv()
        c0 = coord[axes[s][0]]
        for off in (2, 1, 3):
            fifth_copy(s, off, c0).start()

        def move(t, carry):
            es[s, t, pl.ds(pl.multiple_of(c0 * quarter, quarter), quarter)] = ds[s, t]
            return carry

        lax.fori_loop(0, TAPS, move, 0)

    def step_fifth(s):
        c0 = coord[axes[s][0]]
        for off in (1, 2, 3):
            fifth_copy(s, off, lax.rem(c0 + RING - off, RING)).wait_recv()
        last_copy(s).start()
        own_copy(s).start()

    def finish_sum(s):
        last_copy(s).wait()
        own_copy(s).wait()
        pair_copy(s).wait_send()
        for off in (1, 2, 3):
            first_copy(s, off).wait_send()
            second_copy(s, off).wait_send()
            third_copy(s, off, x).wait_send()
            fourth_copy(s, off, coord[axes[s][1]]).wait_send()
            fifth_copy(s, off, coord[axes[s][0]]).wait_send()

    loads[0].wait()
    loads[1].wait()
    side(0, sources[0]).wait_recv()
    conv_inner(xe, w1, acc1, False)
    loads[2].wait()
    loads[3].wait()
    side(1, sources[1]).wait_recv()
    conv_inner(ge, w2, acc2, True)
    pass_corners(0)
    take_faces(0)
    conv_outer(xe, w1, acc1, False)
    each_row(acc1, after_conv1)
    send_faces(2)
    pass_corners(1)
    take_faces(1)
    weight_grad(zt, ge, p2, True)
    pair_copy(0).start()
    conv_outer(ge, w2, acc2, True)
    each_row(acc2, after_conv_g)
    send_faces(3)
    step_pair(0)
    weight_grad(at, xe, p1, False)
    pair_copy(1).start()
    pass_corners(2)
    side(2, sources[2]).wait_recv()
    conv_inner(ze, w2, acc1, False)
    step_pair(1)
    step_first(0)
    side(3, sources[3]).wait_recv()
    conv_inner(ae, w1, acc2, True)
    step_second(0)
    take_faces(2)
    conv_outer(ze, w2, acc1, False)
    step_first(1)
    pass_corners(3)
    each_row(acc1, after_add(xe))
    y_out = pltpu.make_async_copy(obuf, y_hbm, osem.at[0])
    y_out.start()
    step_third(0)
    step_second(1)
    take_faces(3)
    conv_outer(ae, w1, acc2, True)
    step_fourth(0)
    step_third(1)
    y_out.wait()
    each_row(acc2, after_add(ge))
    dx_out = pltpu.make_async_copy(obuf, dx_hbm, osem.at[1])
    dx_out.start()
    step_fourth(1)
    step_fifth(0)
    step_fifth(1)
    dx_out.wait()
    for k in range(4):
        finish_halo(k)
    finish_sum(0)
    finish_sum(1)


def solution(mesh):
    depth_count = mesh.shape["dep"]
    vol_spec = P(None, "dep", "row", None, None)

    def local_step(x_tile, w_conv1, w_conv2, g_tile):
        width = x_tile.shape[3]
        ext = pltpu.VMEM((NB, ND + 2, NH + 2, width, NC), BF16)
        acc = pltpu.VMEM((NB, 6, NH * width, NC), F32)
        trans = pltpu.VMEM((NB * ND * NH, 3 * NC, width), BF16)
        wts = pltpu.VMEM((3, 3, 3, NC, NC), BF16)
        part = pltpu.VMEM((TAPS, NC, NC), F32)
        anywhere = pl.BlockSpec(memory_space=pl.ANY)
        outs = pl.pallas_call(
            functools.partial(kernel, width, depth_count),
            out_shape=(
                jax.ShapeDtypeStruct(x_tile.shape, BF16),
                jax.ShapeDtypeStruct(x_tile.shape, BF16),
                jax.ShapeDtypeStruct((27, NC, NC), F32),
                jax.ShapeDtypeStruct((27, NC, NC), F32),
            ),
            in_specs=[anywhere] * 4,
            out_specs=(anywhere,) * 4,
            scratch_shapes=[
                ext, ext, ext, ext, wts, wts, acc, acc,
                pltpu.VMEM((NB * ND * NH, width, NC), F32),
                trans, trans,
                pltpu.VMEM((NB, ND, NH, width, NC), BF16),
                part, part,
                pltpu.VMEM((2, TAPS, NC // 2, NC), F32),
                pltpu.VMEM((2, RING - 1, TAPS, NC // 8, NC), F32),
                pltpu.VMEM((2, TAPS, NC // 8, NC), F32),
                pltpu.VMEM((2, RING - 1, TQ, NC // 8, NC), F32),
                pltpu.VMEM((2, RING, TQ, NC // 8, NC), F32),
                pltpu.VMEM((2, TAPS, NC // 8, NC), F32),
                pltpu.VMEM((2, TAPS, NC // 2, NC), F32),
                pltpu.SemaphoreType.DMA((4, 4)),
                pltpu.SemaphoreType.DMA((4, 4)),
                pltpu.SemaphoreType.DMA((4, 3)),
                pltpu.SemaphoreType.DMA((4, 3)),
                pltpu.SemaphoreType.DMA((2, 17)),
                pltpu.SemaphoreType.DMA((2, 17)),
                pltpu.SemaphoreType.DMA((4,)),
                pltpu.SemaphoreType.DMA((4,)),
            ],
            compiler_params=pltpu.CompilerParams(collective_id=0, has_side_effects=True, vmem_limit_bytes=66 * 1000 * 1000),
        )(x_tile, w_conv1, w_conv2, g_tile)
        y_tile, dx_tile, dw1, dw2 = outs
        shape = w_conv1.shape
        return (y_tile, dx_tile, dw1.reshape(shape), dw2.reshape(shape))

    return jax.shard_map(local_step, mesh=mesh, in_specs=(vol_spec, P(), P(), vol_spec), out_specs=(vol_spec, vol_spec, P(), P()), check_vma=False)
```

profile of v0, /device:TPU:1, one launch (start us, length us, event | category | flops | bytes accessed | tf_op | source)
XLA Modules:
  0.0 114.6 jit_solution(10654913676732116643)
XLA Ops:
  0.6 107.2 %shard_map.75 = (bf16[2,2,4,256,128]{4,3,2,1,0:T(8,128)(2,1)}, bf16[2,2,4,256,128]{4,3,2,1,0:T(8,128)(2,1)}, f32[27,128,128]{2,1,0:T(8,128)}, f32[27,128,128]{2,1,0:T(8,128)}) custom-call(bf16[2,2,4,256,128]{4,3,2,1,0:T(8,128)(2,1)} %x_hbm.1, bf16[3,3,3,128,128]{4,3,2,1,0:T(8,128)(2,1)} %w1_hbm.1, bf16[3,3,3,128,128]{4,3,2,1,0:T(8,128)(2,1)} %w2_hbm.1, ...), custom_call_target="tpu_custom_call" | custom-call | tf_op jit(solution)/shard_map/pallas_call | solution.py:483
  107.8 0.0 copy-start.2
  107.8 0.0 copy-start.1
  107.8 2.4 %copy.12 = bf16[2,2,4,256,128]{4,3,2,1,0:T(8,128)(2,1)} copy(bf16[2,2,4,256,128]{4,3,2,1,0:T(8,128)(2,1)} %get-tuple-element.16) | data formatting | bytes 2097152
  110.3 0.0 copy-done.2
  110.3 1.0 copy.13
  111.3 0.0 copy-done.1
  111.3 0.0 copy-start
  111.3 1.2 %copy.14 = f32[3,3,3,128,128]{4,3,2,1,0:T(8,128)} copy(f32[3,3,3,128,128]{4,3,2,1,0:T(8,128)S(1)} %bitcast.3) | data formatting | bytes 3538944
  112.5 0.9 copy-done
  113.4 1.2 %copy.15 = f32[3,3,3,128,128]{4,3,2,1,0:T(8,128)} copy(f32[3,3,3,128,128]{4,3,2,1,0:T(8,128)S(1)} %bitcast.2) | data formatting | bytes 3538944
Async XLA Ops:
  107.8 2.5 %copy-start.2 = (bf16[2,2,4,256,128]{4,3,2,1,0:T(8,128)(2,1)S(1)}, bf16[2,2,4,256,128]{4,3,2,1,0:T(8,128)(2,1)}, u32[]{:S(2)}) copy-start(bf16[2,2,4,256,128]{4,3,2,1,0:T(8,128)(2,1)} %get-tuple-element.17) | copy-start | bytes 3145732
  107.8 3.4 %copy-start.1 = (f32[27,128,128]{2,1,0:T(8,128)S(1)}, f32[27,128,128]{2,1,0:T(8,128)}, u32[]{:S(2)}) copy-start(f32[27,128,128]{2,1,0:T(8,128)} %get-tuple-element.10) | copy-start | bytes 5308420
  111.3 2.1 %copy-start = (f32[27,128,128]{2,1,0:T(8,128)S(1)}, f32[27,128,128]{2,1,0:T(8,128)}, u32[]{:S(2)}) copy-start(f32[27,128,128]{2,1,0:T(8,128)} %get-tuple-element.11) | copy-start | bytes 5308420
where the time goes:
time: 115 us
  Pallas kernels  107 us (93%)
  local copies, waits for them, and re-layouts  6.74 us (6%)
    pallas_call x1, Pallas kernels, local_step(): pl.pallas_call(functools.partial(kernel, width, depth_count), out_shape=(...  107 us
    unnamed x10, local copies, waits for them, and re-layouts  6.74 us

commit v1 on v0

--- a/solution.py
+++ b/solution.py
@@ -22,10 +22,10 @@
 
 def kernel(width, depth_count,
            x_hbm, w1_hbm, w2_hbm, g_hbm,
-           y_hbm, dx_hbm, dw1_hbm, dw2_hbm,
-           xe, ge, ze, ae, w1, w2, acc1, acc2, dgel, zt, at, obuf,
-           p2, p1, cr, r1, bz, r2, xb, ds, es,
-           hs_send, hs_recv, rs_send, rs_recv, ar_send, ar_recv, lsem, osem):
+           y_out, dx_out, dw1_out, dw2_out,
+           xe, ge, ze, ae, w1, w2, acc1, acc2, dgel, zt, at,
+           p2, p1, cr, ra, rb, rl, rr, bz, r2, xb, ds,
+           hs_send, hs_recv, rs_send, rs_recv, ar_send, ar_recv, lsem):
     rows = NH * width
     row = lax.axis_index("row")
     dep = lax.axis_index("dep")
@@ -254,12 +254,15 @@
         for tw, v in enumerate((from_right(da), da, from_left(da))):
             at[i, pl.ds(tw * NC, NC)] = v.astype(BF16).T
 
-    def after_add(ext):
+    def after_add(ext, out):
         def use(i, b, d, h, total):
-            obuf[b, d, h] = (total + ext[b, 1 + d, 1 + h].astype(F32)).astype(BF16)
+            out[b, d, h] = (total + ext[b, 1 + d, 1 + h].astype(F32)).astype(BF16)
         return use
 
-    def weight_grad(own_t, ext, part, swap):
+    def tap_index(td, th):
+        return td * 6 + th * 3 if th < 2 else 18 + td * 3
+
+    def weight_grad(own_t, ext, part, swap, between):
         def rhs(td, th):
             d0, h0 = (2 - td, 2 - th) if swap else (td, th)
             return jnp.concatenate([lines(ext, b, d + d0, h0) for b in range(NB) for d in range(ND)], axis=0)
@@ -271,144 +274,172 @@
         def put(out, n, td, th):
             for tw in range(3):
                 blk = out[tw * NC:(tw + 1) * NC, n * NC:(n + 1) * NC]
-                part[td * 9 + th * 3 + tw] = blk if swap else blk.T
-
-        def one(td, carry):
-            out = product(jnp.concatenate([rhs(td, 0), rhs(td, 1)], axis=1))
-            put(out, 0, td, 0)
-            put(out, 1, td, 1)
-            return carry
-
-        lax.fori_loop(0, 3, one, 0)
-        out = product(jnp.concatenate([rhs(0, 2), rhs(1, 2)], axis=1))
-        put(out, 0, 0, 2)
-        put(out, 1, 1, 2)
-        put(product(rhs(2, 2)), 0, 2, 2)
-
-    half, quarter = NC // 2, NC // 8
+                part[tap_index(td, th) + tw] = blk if swap else blk.T
+
+        groups = [((td, 0), (td, 1)) for td in range(3)] + [((0, 2), (1, 2)), ((2, 2),)]
+        for k, taps in enumerate(groups):
+            out = product(jnp.concatenate([rhs(*t) for t in taps], axis=1))
+            for n, t in enumerate(taps):
+                put(out, n, *t)
+            between(k)
+
+    half, piece = NC // 2, NC // 16
     axes = (("y", "z"), ("z", "y"))
     coord = {"x": x, "y": y, "z": z}
     parts = (p2, p1)
-    outs = (dw2_hbm, dw1_hbm)
-
-    def sems(s, n):
-        return ar_send.at[s, n], ar_recv.at[s, n]
-
-    def pair_copy(s):
+    outs = (dw2_out, dw1_out)
+    low, high = pl.ds(0, TAPS // 2), pl.ds(TAPS // 2, TAPS // 2)
+    high27 = pl.ds(TAPS // 2, TAPS // 2 - 1)
+
+    def sems(q, n):
+        return ar_send.at[q, n], ar_recv.at[q, n]
+
+    def turn(c, off):
+        return lax.rem(c + off, RING)
+
+    def chunk(q, off):
+        c = turn(coord[axes[q % 2][0]], off)
+        return pl.ds(pl.multiple_of(row * half + (q % 2) * (half // 2) + c * piece, piece), piece)
+
+    def pair_copy(s, n):
         theirs = pl.ds(pl.multiple_of(other * half, half), half)
-        return rdma(parts[s].at[:, theirs], cr.at[s], *sems(s, 0), (other, dep))
-
-    def first_copy(s, off):
-        axis = axes[s][0]
-        j = lax.rem(coord[axis] + off, RING)
-        src = parts[s].at[:, pl.ds(pl.multiple_of(row * half + j * quarter, quarter), quarter)]
-        return rdma(src, r1.at[s, off - 1], *sems(s, off), (row, ring_dep(axis, off)))
-
-    def second_copy(s, off):
-        axis = axes[s][1]
-        j = lax.rem(coord[axis] + off, RING)
-        return rdma(bz.at[s, pl.ds(j * TQ, TQ)], r2.at[s, off - 1], *sems(s, 3 + off), (row, ring_dep(axis, off)))
-
-    def third_copy(s, off, slot):
-        return rdma(xb.at[s, slot], xb.at[s, slot], *sems(s, 6 + off), (row, ring_dep("x", off)))
-
-    def fourth_copy(s, off, j):
-        axis = axes[s][1]
-        return rdma(ds.at[s, pl.ds(j * TQ, TQ)], ds.at[s, pl.ds(j * TQ, TQ)], *sems(s, 9 + off), (row, ring_dep(axis, off)))
-
-    def fifth_copy(s, off, j):
-        axis = axes[s][0]
-        return rdma(ds.at[s], es.at[s, :, pl.ds(pl.multiple_of(j * quarter, quarter), quarter)], *sems(s, 12 + off), (row, ring_dep(axis, off)))
+        taps = pl.ds(0, 18) if n == 0 else pl.ds(18, TAPS - 18)
+        return rdma(parts[s].at[taps, theirs], cr.at[s, taps], *sems(2 * s + n, 22), (other, dep))
+
+    def scatter_copy(q, n):
+        part = parts[q // 2]
+        nxt, prv = (row, ring_dep(axes[q % 2][0], 1)), (row, ring_dep(axes[q % 2][0], RING - 1))
+        src, dst, dev = (
+            (part.at[low, chunk(q, 2)], ra.at[q], nxt),
+            (part.at[high, chunk(q, 2)], rb.at[q], prv),
+            (part.at[high, chunk(q, 1)], rl.at[q, high], nxt),
+            (part.at[low, chunk(q, 3)], rr.at[q, low], prv),
+            (ra.at[q], rl.at[q, low], nxt),
+            (rb.at[q], rr.at[q, high], prv),
+        )[n]
+        return rdma(src, dst, *sems(q, n), dev)
+
+    def second_copy(q, off):
+        axis = axes[q % 2][1]
+        j = turn(coord[axis], off)
+        return rdma(bz.at[q, pl.ds(j * TQ, TQ)], r2.at[q, off - 1], *sems(q, 5 + off), (row, ring_dep(axis, off)))
+
+    def third_copy(q, off, slot):
+        return rdma(xb.at[q, slot], xb.at[q, slot], *sems(q, 8 + off), (row, ring_dep("x", off)))
+
+    def fourth_copy(q, off, j):
+        return rdma(ds.at[q, pl.ds(j * TQ, TQ)], ds.at[q, pl.ds(j * TQ, TQ)], *sems(q, 11 + off), (row, ring_dep(axes[q % 2][1], off)))
+
+    def gather_copy(q, n):
+        out = outs[q // 2]
+        nxt, prv = (row, ring_dep(axes[q % 2][0], 1)), (row, ring_dep(axes[q % 2][0], RING - 1))
+        taps, off, dev = (
+            (low, 0, nxt),
+            (high27, 0, prv),
+            (high27, 0, nxt),
+            (low, 0, prv),
+            (low, 3, nxt),
+            (high27, 1, prv),
+        )[n]
+        src = ds.at[q, taps] if n < 4 else out.at[taps, chunk(q, off)]
+        return rdma(src, out.at[taps, chunk(q, off)], *sems(q, 15 + n), dev)
+
+    def last_copy(q):
+        rows_q = pl.ds(pl.multiple_of(row * half + (q % 2) * (half // 2), half // 2), half // 2)
+        return rdma(outs[q // 2].at[:, rows_q], outs[q // 2].at[:, rows_q], *sems(q, 21), (other, dep))
 
     my_half = pl.ds(pl.multiple_of(row * half, half), half)
 
-    def last_copy(s):
-        return rdma(es.at[s, pl.ds(0, 27)], outs[s].at[:, my_half], *sems(s, 16), (other, dep))
-
-    def own_copy(s):
-        return pltpu.make_async_copy(es.at[s, pl.ds(0, 27)], outs[s].at[:, my_half], osem.at[2 + s])
-
     def step_pair(s):
-        pair_copy(s).wait_recv()
+        pair_copy(s, 0).wait_recv()
+        pair_copy(s, 1).wait_recv()
 
         def add(t, carry):
             parts[s][t, my_half] += cr[s, t]
             return carry
 
         lax.fori_loop(0, TAPS, add, 0)
+        for n in range(4):
+            for u in range(2):
+                scatter_copy(2 * s + u, n).start()
+
+    def step_relay(q):
+        part = parts[q // 2]
+        to_next, to_prev = chunk(q, 1), chunk(q, 3)
+        scatter_copy(q, 0).wait_recv()
+        ra[q] += part[low, to_next]
+        scatter_copy(q, 4).start()
+        scatter_copy(q, 1).wait_recv()
+        rb[q] += part[high, to_prev]
+        scatter_copy(q, 5).start()
+
+    def step_first(q):
+        for n in range(2, 6):
+            scatter_copy(q, n).wait_recv()
+        bz[q] = parts[q // 2][:, chunk(q, 0)] + (rl[q] + rr[q])
         for off in (2, 1, 3):
-            first_copy(s, off).start()
-
-    def step_first(s):
+            second_copy(q, off).start()
+
+    def step_second(q):
         for off in (1, 2, 3):
-            first_copy(s, off).wait_recv()
-        mine = pl.ds(pl.multiple_of(row * half + coord[axes[s][0]] * quarter, quarter), quarter)
-
-        def add(t, carry):
-            bz[s, t] = (parts[s][t, mine] + r1[s, 0, t]) + (r1[s, 1, t] + r1[s, 2, t])
-            return carry
-
-        lax.fori_loop(0, TAPS, add, 0)
+            second_copy(q, off).wait_recv()
+        c = coord[axes[q % 2][1]]
+        xb[q, x] = (bz[q, pl.ds(c * TQ, TQ)] + r2[q, 0]) + (r2[q, 1] + r2[q, 2])
         for off in (2, 1, 3):
-            second_copy(s, off).start()
-
-    def step_second(s):
+            third_copy(q, off, x).start()
+
+    def step_third(q):
         for off in (1, 2, 3):
-            second_copy(s, off).wait_recv()
-        c = coord[axes[s][1]]
-
-        def add(t, carry):
-            xb[s, x, t] = (bz[s, c * TQ + t] + r2[s, 0, t]) + (r2[s, 1, t] + r2[s, 2, t])
-            return carry
-
-        lax.fori_loop(0, TQ, add, 0)
+            third_copy(q, off, turn(x, RING - off)).wait_recv()
+        c = coord[axes[q % 2][1]]
+        ds[q, pl.ds(c * TQ, TQ)] = (xb[q, 0] + xb[q, 1]) + (xb[q, 2] + xb[q, 3])
         for off in (2, 1, 3):
-            third_copy(s, off, x).start()
-
-    def step_third(s):
+            fourth_copy(q, off, c).start()
+
+    def step_fourth(q):
+        c = coord[axes[q % 2][1]]
         for off in (1, 2, 3):
-            third_copy(s, off, lax.rem(x + RING - off, RING)).wait_recv()
-        c = coord[axes[s][1]]
-
-        def add(t, carry):
-            ds[s, c * TQ + t] = (xb[s, 0, t] + xb[s, 1, t]) + (xb[s, 2, t] + xb[s, 3, t])
-            return carry
-
-        lax.fori_loop(0, TQ, add, 0)
-        for off in (2, 1, 3):
-            fourth_copy(s, off, c).start()
-
-    def step_fourth(s):
-        c = coord[axes[s][1]]
+            fourth_copy(q, off, turn(c, RING - off)).wait_recv()
+        for n in range(4):
+            gather_copy(q, n).start()
+        outs[q // 2][:, chunk(q, 0)] = ds[q, pl.ds(0, 27)]
+
+    def step_forward(q):
+        gather_copy(q, 0).wait_recv()
+        gather_copy(q, 4).start()
+        gather_copy(q, 1).wait_recv()
+        gather_copy(q, 5).start()
+
+    def step_fifth(q):
+        for n in range(2, 6):
+            gather_copy(q, n).wait_recv()
+        last_copy(q).start()
+
+    def finish_sum(q):
+        last_copy(q).wait()
+        pair_copy(q // 2, q % 2).wait_send()
+        for n in range(6):
+            scatter_copy(q, n).wait_send()
+            gather_copy(q, n).wait_send()
         for off in (1, 2, 3):
-            fourth_copy(s, off, lax.rem(c + RING - off, RING)).wait_recv()
-        c0 = coord[axes[s][0]]
-        for off in (2, 1, 3):
-            fifth_copy(s, off, c0).start()
-
-        def move(t, carry):
-            es[s, t, pl.ds(pl.multiple_of(c0 * quarter, quarter), quarter)] = ds[s, t]
-            return carry
-
-        lax.fori_loop(0, TAPS, move, 0)
-
-    def step_fifth(s):
-        c0 = coord[axes[s][0]]
-        for off in (1, 2, 3):
-            fifth_copy(s, off, lax.rem(c0 + RING - off, RING)).wait_recv()
-        last_copy(s).start()
-        own_copy(s).start()
-
-    def finish_sum(s):
-        last_copy(s).wait()
-        own_copy(s).wait()
-        pair_copy(s).wait_send()
-        for off in (1, 2, 3):
-            first_copy(s, off).wait_send()
-            second_copy(s, off).wait_send()
-            third_copy(s, off, x).wait_send()
-            fourth_copy(s, off, coord[axes[s][1]]).wait_send()
-            fifth_copy(s, off, coord[axes[s][0]]).wait_send()
+            second_copy(q, off).wait_send()
+            third_copy(q, off, x).wait_send()
+            fourth_copy(q, off, coord[axes[q % 2][1]]).wait_send()
+
+    def after_dw2(k):
+        if k == 2:
+            pair_copy(0, 0).start()
+        if k == 4:
+            pair_copy(0, 1).start()
+
+    def after_dw1(k):
+        if k == 1:
+            step_relay(0)
+            step_relay(1)
+        if k == 2:
+            pair_copy(1, 0).start()
+        if k == 4:
+            pair_copy(1, 1).start()
 
     loads[0].wait()
     loads[1].wait()
@@ -424,48 +455,69 @@
     each_row(acc1, after_conv1)
     send_faces(2)
     pass_corners(1)
+    side(2, sources[2]).wait_recv()
+    conv_inner(ze, w2, acc1, False)
     take_faces(1)
-    weight_grad(zt, ge, p2, True)
-    pair_copy(0).start()
+    weight_grad(zt, ge, p2, True, after_dw2)
     conv_outer(ge, w2, acc2, True)
+    step_pair(0)
     each_row(acc2, after_conv_g)
     send_faces(3)
-    step_pair(0)
-    weight_grad(at, xe, p1, False)
-    pair_copy(1).start()
+    weight_grad(at, xe, p1, False, after_dw1)
     pass_corners(2)
-    side(2, sources[2]).wait_recv()
-    conv_inner(ze, w2, acc1, False)
+    step_first(0)
+    step_first(1)
     step_pair(1)
-    step_first(0)
+    take_faces(2)
+    conv_outer(ze, w2, acc1, False)
+    step_second(0)
+    step_second(1)
+    each_row(acc1, after_add(xe, y_out))
+    step_relay(2)
+    step_relay(3)
     side(3, sources[3]).wait_recv()
     conv_inner(ae, w1, acc2, True)
-    step_second(0)
-    take_faces(2)
-    conv_outer(ze, w2, acc1, False)
-    step_first(1)
+    step_third(0)
+    step_third(1)
+    step_first(2)
+    step_first(3)
     pass_corners(3)
-    each_row(acc1, after_add(xe))
-    y_out = pltpu.make_async_copy(obuf, y_hbm, osem.at[0])
-    y_out.start()
-    step_third(0)
-    step_second(1)
     take_faces(3)
     conv_outer(ae, w1, acc2, True)
+    each_row(acc2, after_add(ge, dx_out))
     step_fourth(0)
-    step_third(1)
-    y_out.wait()
-    each_row(acc2, after_add(ge))
-    dx_out = pltpu.make_async_copy(obuf, dx_hbm, osem.at[1])
-    dx_out.start()
     step_fourth(1)
+    step_second(2)
+    step_second(3)
+    step_forward(0)
+    step_forward(1)
+    step_third(2)
+    step_third(3)
     step_fifth(0)
     step_fifth(1)
-    dx_out.wait()
+    step_fourth(2)
+    step_fourth(3)
+    step_forward(2)
+    step_forward(3)
+    step_fifth(2)
+    step_fifth(3)
     for k in range(4):
         finish_halo(k)
-    finish_sum(0)
-    finish_sum(1)
+    for q in range(4):
+        finish_sum(q)
+
+
+def to_hbm(y_vm, dx_vm, dw1_vm, dw2_vm, y_hbm, dx_hbm, dw1_hbm, dw2_hbm, sem):
+    copies = [(y_vm, y_hbm), (dx_vm, dx_hbm)]
+    for src, dst in ((dw1_vm, dw1_hbm), (dw2_vm, dw2_hbm)):
+        for td in range(3):
+            copies.append((src.at[pl.ds(td * 6, 6)], dst.at[pl.ds(td * 9, 6)]))
+            copies.append((src.at[pl.ds(18 + td * 3, 3)], dst.at[pl.ds(td * 9 + 6, 3)]))
+    started = [pltpu.make_async_copy(src, dst, sem.at[n]) for n, (src, dst) in enumerate(copies)]
+    for copy in started:
+        copy.start()
+    for copy in started:
+        copy.wait()
 
 
 def solution(mesh):
@@ -483,38 +535,50 @@
         outs = pl.pallas_call(
             functools.partial(kernel, width, depth_count),
             out_shape=(
+                pltpu.VMEM(x_tile.shape, BF16),
+                pltpu.VMEM(x_tile.shape, BF16),
+                pltpu.VMEM((27, NC, NC), F32),
+                pltpu.VMEM((27, NC, NC), F32),
+            ),
+            in_specs=[anywhere] * 4,
+            out_specs=(pl.BlockSpec(memory_space=pltpu.VMEM),) * 4,
+            scratch_shapes=[
+                ext, ext, ext, ext, wts, wts, acc, acc,
+                pltpu.VMEM((NB * ND * NH, width, NC), F32),
+                trans, trans,
+                part, part,
+                pltpu.VMEM((2, TAPS, NC // 2, NC), F32),
+                pltpu.VMEM((4, TAPS // 2, NC // 16, NC), F32),
+                pltpu.VMEM((4, TAPS // 2, NC // 16, NC), F32),
+                pltpu.VMEM((4, TAPS, NC // 16, NC), F32),
+                pltpu.VMEM((4, TAPS, NC // 16, NC), F32),
+                pltpu.VMEM((4, TAPS, NC // 16, NC), F32),
+                pltpu.VMEM((4, RING - 1, TQ, NC // 16, NC), F32),
+                pltpu.VMEM((4, RING, TQ, NC // 16, NC), F32),
+                pltpu.VMEM((4, TAPS, NC // 16, NC), F32),
+                pltpu.SemaphoreType.DMA((4, 4)),
+                pltpu.SemaphoreType.DMA((4, 4)),
+                pltpu.SemaphoreType.DMA((4, 3)),
+                pltpu.SemaphoreType.DMA((4, 3)),
+                pltpu.SemaphoreType.DMA((4, 23)),
+                pltpu.SemaphoreType.DMA((4, 23)),
+                pltpu.SemaphoreType.DMA((4,)),
+            ],
+            compiler_params=pltpu.CompilerParams(collective_id=0, has_side_effects=True, vmem_limit_bytes=56 * 1000 * 1000),
+        )(x_tile, w_conv1, w_conv2, g_tile)
+        y_tile, dx_tile, dw1, dw2 = pl.pallas_call(
+            to_hbm,
+            out_shape=(
                 jax.ShapeDtypeStruct(x_tile.shape, BF16),
                 jax.ShapeDtypeStruct(x_tile.shape, BF16),
                 jax.ShapeDtypeStruct((27, NC, NC), F32),
                 jax.ShapeDtypeStruct((27, NC, NC), F32),
             ),
-            in_specs=[anywhere] * 4,
+            in_specs=[pl.BlockSpec(memory_space=pltpu.VMEM)] * 4,
             out_specs=(anywhere,) * 4,
-            scratch_shapes=[
-                ext, ext, ext, ext, wts, wts, acc, acc,
-                pltpu.VMEM((NB * ND * NH, width, NC), F32),
-                trans, trans,
-                pltpu.VMEM((NB, ND, NH, width, NC), BF16),
-                part, part,
-                pltpu.VMEM((2, TAPS, NC // 2, NC), F32),
-                pltpu.VMEM((2, RING - 1, TAPS, NC // 8, NC), F32),
-                pltpu.VMEM((2, TAPS, NC // 8, NC), F32),
-                pltpu.VMEM((2, RING - 1, TQ, NC // 8, NC), F32),
-                pltpu.VMEM((2, RING, TQ, NC // 8, NC), F32),
-                pltpu.VMEM((2, TAPS, NC // 8, NC), F32),
-                pltpu.VMEM((2, TAPS, NC // 2, NC), F32),
-                pltpu.SemaphoreType.DMA((4, 4)),
-                pltpu.SemaphoreType.DMA((4, 4)),
-                pltpu.SemaphoreType.DMA((4, 3)),
-                pltpu.SemaphoreType.DMA((4, 3)),
-                pltpu.SemaphoreType.DMA((2, 17)),
-                pltpu.SemaphoreType.DMA((2, 17)),
-                pltpu.SemaphoreType.DMA((4,)),
-                pltpu.SemaphoreType.DMA((4,)),
-            ],
-            compiler_params=pltpu.CompilerParams(collective_id=0, has_side_effects=True, vmem_limit_bytes=66 * 1000 * 1000),
-        )(x_tile, w_conv1, w_conv2, g_tile)
-        y_tile, dx_tile, dw1, dw2 = outs
+            scratch_shapes=[pltpu.SemaphoreType.DMA((14,))],
+            compiler_params=pltpu.CompilerParams(vmem_limit_bytes=4 * 1000 * 1000),
+        )(*outs)
         shape = w_conv1.shape
         return (y_tile, dx_tile, dw1.reshape(shape), dw2.reshape(shape))
 

time: 115 us -> 97.9 us (0.85)
  Pallas kernels: 107 us -> 97 us
  local copies, waits for them, and re-layouts: 6.74 us -> 0 us
    pallas_call x1, Pallas kernels: 107 us -> 94.5 us  [local_step(): pl.pallas_call(functools.partial(kernel, width, depth_count), out_shape=(...]
    unnamed x10 -> x0, local copies, waits for them, and re-layouts: 6.74 us -> none
    pallas_call x0 -> x1, Pallas kernels: none -> 2.56 us  [local_step(): pl.pallas_call(to_hbm, out_shape=(jax.ShapeDtypeStruct(x_tile.shape, BF16...]
where the time goes in v1:
time: 97.9 us; the launch traced here: 97.8 us
  Pallas kernels  97 us (99%)
    pallas_call x1, Pallas kernels, local_step(): pl.pallas_call(functools.partial(kernel, width, depth_count), out_shape=(...  94.5 us
    pallas_call x1, Pallas kernels, local_step(): pl.pallas_call(to_hbm, out_shape=(jax.ShapeDtypeStruct(x_tile.shape, BF16...  2.56 us

profile of v1, /device:TPU:1, one launch (start us, length us, event | category | flops | bytes accessed | tf_op | source)
XLA Modules:
  0.0 97.8 jit_solution(10079362404693672412)
XLA Ops:
  0.6 94.5 %shard_map.75 = (bf16[2,2,4,256,128]{4,3,2,1,0:T(8,128)(2,1)S(1)}, bf16[2,2,4,256,128]{4,3,2,1,0:T(8,128)(2,1)S(1)}, f32[27,128,128]{2,1,0:T(8,128)S(1)}, f32[27,128,128]{2,1,0:T(8,128)S(1)}) custom-call(bf16[2,2,4,256,128]{4,3,2,1,0:T(8,128)(2,1)} %x_hbm.1, bf16[3,3,3,128,128]{4,3,2,1,0:T(8,128)(2,1)} %w1_hbm.1, bf16[3,3,3,128,128]{4,3,2,1,0:T(8,128)(2,1)} %w2_hbm.1, ...), custom_call_target="tpu_custom_call" | custom-call | tf_op jit(solution)/shard_map/pallas_call | solution.py:535
  95.1 2.6 %shard_map.76 = (bf16[2,2,4,256,128]{4,3,2,1,0:T(8,128)(2,1)}, bf16[2,2,4,256,128]{4,3,2,1,0:T(8,128)(2,1)}, f32[27,128,128]{2,1,0:T(8,128)}, f32[27,128,128]{2,1,0:T(8,128)}) custom-call(bf16[2,2,4,256,128]{4,3,2,1,0:T(8,128)(2,1)S(1)} %get-tuple-element.12.y_vm, bf16[2,2,4,256,128]{4,3,2,1,0:T(8,128)(2,1)S(1)} %get-tuple-element.13.dx_vm, ...), custom_call_target="tpu_custom_call" | custom-call | tf_op jit(solution)/shard_map/pallas_call | solution.py:569

commit v2 on v1

--- a/solution.py
+++ b/solution.py
@@ -24,8 +24,8 @@
            x_hbm, w1_hbm, w2_hbm, g_hbm,
            y_out, dx_out, dw1_out, dw2_out,
            xe, ge, ze, ae, w1, w2, acc1, acc2, dgel, zt, at,
-           p2, p1, cr, ra, rb, rl, rr, bz, r2, xb, ds,
-           hs_send, hs_recv, rs_send, rs_recv, ar_send, ar_recv, lsem):
+           p2, p1, cr, ra, rb, rl, rr, bz, r2, xb, ds, hold,
+           hs_send, hs_recv, rs_send, rs_recv, ar_send, ar_recv, hold_send, hold_recv, lsem):
     rows = NH * width
     row = lax.axis_index("row")
     dep = lax.axis_index("dep")
@@ -49,6 +49,8 @@
 
     has_below = dep > 0
     has_above = dep < depth_count - 1
+    near_above, near_below = x < RING - 1, x > 0
+    far_above, far_below = has_above & (x == RING - 1), has_below & (x == 0)
 
     def face(k, src_of, up, part):
         h0, hn = (edge, 1) if part == 0 else (row, NH - 1)
@@ -77,16 +79,54 @@
 
     sources = (from_hbm(x_hbm), from_hbm(g_hbm), from_ext(ze), from_ext(ae))
 
-    def send_faces(k):
-        side(k, sources[k]).start()
+    def send_faces(k, above, below):
         for part in range(2):
-            @pl.when(has_above)
+            @pl.when(above)
             def _():
                 face(k, sources[k], True, part).start()
 
-            @pl.when(has_below)
+            @pl.when(below)
             def _():
                 face(k, sources[k], False, part).start()
+
+    split = (2, 3)
+    relays_up, relays_down = (x == RING - 1) & (dep >= RING), (x == 0) & (dep < depth_count - RING)
+
+    def far_row(k, up):
+        d_src, d_dst = (ND - 1, 0) if up else (0, ND + 1)
+        dev = (row, dep + 1) if up else (row, dep - 1)
+        n = 4 if up else 5
+        return rdma(sources[k](d_src, row, 1), exts[k].at[:, d_dst, pl.ds(1 + row, 1)], hs_send.at[k, n], hs_recv.at[k, n], dev)
+
+    def far_hop(k, up):
+        dev = (row, dep + RING) if up else (row, dep - RING)
+        return rdma(sources[k](ND - 1 if up else 0, row + 1, 2), hold.at[k - 2], hold_send.at[k - 2], hold_recv.at[k - 2], dev)
+
+    def far_land(k, up):
+        d_dst = 0 if up else ND + 1
+        dev = (row, dep - (RING - 1)) if up else (row, dep + (RING - 1))
+        n = 6 if up else 7
+        return rdma(hold.at[k - 2], exts[k].at[:, d_dst, pl.ds(2 + row, 2)], hs_send.at[k, n], hs_recv.at[k, n], dev)
+
+    def send_far_faces(k):
+        for up, cond in ((True, far_above), (False, far_below)):
+            @pl.when(cond)
+            def _():
+                face(k, sources[k], up, 0).start()
+                far_row(k, up).start()
+
+    def send_far_hops(k):
+        for up, cond in ((True, far_above), (False, far_below)):
+            @pl.when(cond)
+            def _():
+                far_hop(k, up).start()
+
+    def relay_far(k):
+        for up, cond in ((True, relays_up), (False, relays_down)):
+            @pl.when(cond)
+            def _():
+                far_hop(k, up).wait_recv()
+                far_land(k, up).start()
 
     def pass_corners(k):
         @pl.when(has_below)
@@ -100,26 +140,43 @@
             corner(k, False).start()
 
     def take_faces(k):
-        @pl.when(has_below)
-        def _():
-            face(k, sources[k], True, 1).wait_recv()
-            corner(k, True).wait_recv()
-
-        @pl.when(has_above)
-        def _():
-            face(k, sources[k], False, 1).wait_recv()
-            corner(k, False).wait_recv()
+        for up, has, whole in ((True, has_below, x > 0), (False, has_above, x < RING - 1)):
+            @pl.when(has)
+            def _():
+                corner(k, up).wait_recv()
+
+            @pl.when(has if k not in split else has & whole)
+            def _():
+                face(k, sources[k], up, 1).wait_recv()
+
+            if k in split:
+                @pl.when(has & jnp.logical_not(whole))
+                def _():
+                    far_row(k, up).wait_recv()
+                    far_land(k, up).wait_recv()
 
     def finish_halo(k):
         side(k, sources[k]).wait_send()
-        for part in range(2):
-            @pl.when(has_above)
-            def _():
-                face(k, sources[k], True, part).wait_send()
-
-            @pl.when(has_below)
-            def _():
-                face(k, sources[k], False, part).wait_send()
+        for up, has, far, whole in ((True, has_above, far_above, near_above), (False, has_below, far_below, near_below)):
+            @pl.when(has)
+            def _():
+                face(k, sources[k], up, 0).wait_send()
+
+            @pl.when(has if k not in split else whole)
+            def _():
+                face(k, sources[k], up, 1).wait_send()
+
+            if k in split:
+                @pl.when(far)
+                def _():
+                    far_row(k, up).wait_send()
+                    far_hop(k, up).wait_send()
+
+        if k in split:
+            for up, cond in ((True, relays_up), (False, relays_down)):
+                @pl.when(cond)
+                def _():
+                    far_land(k, up).wait_send()
 
         @pl.when(has_below)
         def _():
@@ -135,7 +192,7 @@
         for off in range(1, RING):
             pl.semaphore_signal(barrier, inc=1, device_id=(row, ring_dep(axis, off)), device_id_type=MESH)
 
-    for step in (1, depth_count - 1):
+    for step in (1, depth_count - 1, RING, depth_count - RING):
         pl.semaphore_signal(barrier, inc=1, device_id=(row, lax.rem(dep + step, depth_count)), device_id_type=MESH)
 
     loads = [
@@ -147,10 +204,11 @@
     for load in loads:
         load.start()
 
-    pl.semaphore_wait(barrier, 12)
-
-    send_faces(0)
-    send_faces(1)
+    pl.semaphore_wait(barrier, 14)
+
+    for k in range(2):
+        side(k, sources[k]).start()
+        send_faces(k, has_above, has_below)
 
     zero_row = jnp.zeros((NB, 1, width, NC), BF16)
     for ext in exts:
@@ -189,7 +247,7 @@
     def mul(lhs, rhs, flip):
         return lax.dot_general(lhs, rhs, (((1,), (1 if flip else 0,)), ((), ())), preferred_element_type=F32)
 
-    def conv_inner(ext, w, acc, flip):
+    def conv_inner(ext, w, acc, flip, b0=0, b1=NB):
         cells = []
         for dd in (1, 2):
             for th in range(3):
@@ -205,7 +263,7 @@
                     acc[b, d * 3 + tw] = out[:, j * NC:(j + 1) * NC]
             return carry
 
-        lax.fori_loop(0, NB, one, 0)
+        lax.fori_loop(b0, b1, one, 0)
 
     def conv_outer(ext, w, acc, flip):
         def one(i, carry):
@@ -304,7 +362,7 @@
     def pair_copy(s, n):
         theirs = pl.ds(pl.multiple_of(other * half, half), half)
         taps = pl.ds(0, 18) if n == 0 else pl.ds(18, TAPS - 18)
-        return rdma(parts[s].at[taps, theirs], cr.at[s, taps], *sems(2 * s + n, 22), (other, dep))
+        return rdma(parts[s].at[taps, theirs], cr.at[s, taps], *sems(2 * s + n, 26), (other, dep))
 
     def scatter_copy(q, n):
         part = parts[q // 2]
@@ -344,9 +402,11 @@
         src = ds.at[q, taps] if n < 4 else out.at[taps, chunk(q, off)]
         return rdma(src, out.at[taps, chunk(q, off)], *sems(q, 15 + n), dev)
 
-    def last_copy(q):
-        rows_q = pl.ds(pl.multiple_of(row * half + (q % 2) * (half // 2), half // 2), half // 2)
-        return rdma(outs[q // 2].at[:, rows_q], outs[q // 2].at[:, rows_q], *sems(q, 21), (other, dep))
+    def out_copy(q, n):
+        out = outs[q // 2]
+        taps, off = ((pl.ds(0, 27), 0), (pl.ds(0, 27), 3), (pl.ds(0, 27), 1), (low, 2), (high27, 2))[n]
+        src = ds.at[q, taps] if n == 0 else out.at[taps, chunk(q, off)]
+        return rdma(src, out.at[taps, chunk(q, off)], *sems(q, 21 + n), (other, dep))
 
     my_half = pl.ds(pl.multiple_of(row * half, half), half)
 
@@ -402,6 +462,7 @@
             fourth_copy(q, off, turn(c, RING - off)).wait_recv()
         for n in range(4):
             gather_copy(q, n).start()
+        out_copy(q, 0).start()
         outs[q // 2][:, chunk(q, 0)] = ds[q, pl.ds(0, 27)]
 
     def step_forward(q):
@@ -413,10 +474,11 @@
     def step_fifth(q):
         for n in range(2, 6):
             gather_copy(q, n).wait_recv()
-        last_copy(q).start()
+            out_copy(q, n - 1).start()
 
     def finish_sum(q):
-        last_copy(q).wait()
+        for n in range(5):
+            out_copy(q, n).wait()
         pair_copy(q // 2, q % 2).wait_send()
         for n in range(6):
             scatter_copy(q, n).wait_send()
@@ -433,11 +495,10 @@
             pair_copy(0, 1).start()
 
     def after_dw1(k):
-        if k == 1:
+        if k == 2:
+            pair_copy(1, 0).start()
             step_relay(0)
             step_relay(1)
-        if k == 2:
-            pair_copy(1, 0).start()
         if k == 4:
             pair_copy(1, 1).start()
 
@@ -453,50 +514,59 @@
     take_faces(0)
     conv_outer(xe, w1, acc1, False)
     each_row(acc1, after_conv1)
-    send_faces(2)
+    side(2, sources[2]).start()
+    send_faces(2, near_above, near_below)
+    send_far_faces(2)
+    send_far_hops(2)
     pass_corners(1)
     side(2, sources[2]).wait_recv()
     conv_inner(ze, w2, acc1, False)
     take_faces(1)
     weight_grad(zt, ge, p2, True, after_dw2)
+    relay_far(2)
     conv_outer(ge, w2, acc2, True)
     step_pair(0)
     each_row(acc2, after_conv_g)
-    send_faces(3)
+    side(3, sources[3]).start()
+    send_faces(3, near_above, near_below)
+    send_far_faces(3)
+    send_far_hops(3)
     weight_grad(at, xe, p1, False, after_dw1)
     pass_corners(2)
+    step_pair(1)
     step_first(0)
     step_first(1)
-    step_pair(1)
     take_faces(2)
     conv_outer(ze, w2, acc1, False)
+    relay_far(3)
+    step_relay(2)
+    step_relay(3)
     step_second(0)
     step_second(1)
     each_row(acc1, after_add(xe, y_out))
-    step_relay(2)
-    step_relay(3)
     side(3, sources[3]).wait_recv()
-    conv_inner(ae, w1, acc2, True)
+    conv_inner(ae, w1, acc2, True, 0, 1)
+    step_first(2)
+    step_first(3)
     step_third(0)
     step_third(1)
-    step_first(2)
-    step_first(3)
     pass_corners(3)
+    conv_inner(ae, w1, acc2, True, 1, 2)
+    step_second(2)
+    step_second(3)
+    step_fourth(0)
+    step_fourth(1)
     take_faces(3)
     conv_outer(ae, w1, acc2, True)
-    each_row(acc2, after_add(ge, dx_out))
-    step_fourth(0)
-    step_fourth(1)
-    step_second(2)
-    step_second(3)
+    step_third(2)
+    step_third(3)
     step_forward(0)
     step_forward(1)
-    step_third(2)
-    step_third(3)
+    each_row(acc2, after_add(ge, dx_out))
+    step_fourth(2)
+    step_fourth(3)
     step_fifth(0)
     step_fifth(1)
-    step_fourth(2)
-    step_fourth(3)
     step_forward(2)
     step_forward(3)
     step_fifth(2)
@@ -556,12 +626,15 @@
                 pltpu.VMEM((4, RING - 1, TQ, NC // 16, NC), F32),
                 pltpu.VMEM((4, RING, TQ, NC // 16, NC), F32),
                 pltpu.VMEM((4, TAPS, NC // 16, NC), F32),
-                pltpu.SemaphoreType.DMA((4, 4)),
-                pltpu.SemaphoreType.DMA((4, 4)),
+                pltpu.VMEM((2, NB, 2, width, NC), BF16),
+                pltpu.SemaphoreType.DMA((4, 8)),
+                pltpu.SemaphoreType.DMA((4, 8)),
                 pltpu.SemaphoreType.DMA((4, 3)),
                 pltpu.SemaphoreType.DMA((4, 3)),
-                pltpu.SemaphoreType.DMA((4, 23)),
-                pltpu.SemaphoreType.DMA((4, 23)),
+                pltpu.SemaphoreType.DMA((4, 27)),
+                pltpu.SemaphoreType.DMA((4, 27)),
+                pltpu.SemaphoreType.DMA((2,)),
+                pltpu.SemaphoreType.DMA((2,)),
                 pltpu.SemaphoreType.DMA((4,)),
             ],
             compiler_params=pltpu.CompilerParams(collective_id=0, has_side_effects=True, vmem_limit_bytes=56 * 1000 * 1000),

time: 97.9 us -> 92.3 us (0.943)
  Pallas kernels: 97 us -> 91.4 us
    pallas_call x1, Pallas kernels: 94.5 us -> 88.8 us  [local_step(): pl.pallas_call(functools.partial(kernel, width, depth_count), out_shape=(...]
where the time goes in v2:
time: 92.3 us; the launch traced here: 92.2 us
  Pallas kernels  91.4 us (99%)
    pallas_call x1, Pallas kernels, local_step(): pl.pallas_call(functools.partial(kernel, width, depth_count), out_shape=(...  88.8 us
    pallas_call x1, Pallas kernels, local_step(): pl.pallas_call(to_hbm, out_shape=(jax.ShapeDtypeStruct(x_tile.shape, BF16...  2.56 us

profile of v2, /device:TPU:1, one launch (start us, length us, event | category | flops | bytes accessed | tf_op | source)
XLA Modules:
  0.0 92.2 jit_solution(16648177012034385156)
XLA Ops:
  0.6 88.8 %shard_map.75 = (bf16[2,2,4,256,128]{4,3,2,1,0:T(8,128)(2,1)S(1)}, bf16[2,2,4,256,128]{4,3,2,1,0:T(8,128)(2,1)S(1)}, f32[27,128,128]{2,1,0:T(8,128)S(1)}, f32[27,128,128]{2,1,0:T(8,128)S(1)}) custom-call(bf16[2,2,4,256,128]{4,3,2,1,0:T(8,128)(2,1)} %x_hbm.1, bf16[3,3,3,128,128]{4,3,2,1,0:T(8,128)(2,1)} %w1_hbm.1, bf16[3,3,3,128,128]{4,3,2,1,0:T(8,128)(2,1)} %w2_hbm.1, ...), custom_call_target="tpu_custom_call" | custom-call | tf_op jit(solution)/shard_map/pallas_call | solution.py:605
  89.5 2.6 %shard_map.76 = (bf16[2,2,4,256,128]{4,3,2,1,0:T(8,128)(2,1)}, bf16[2,2,4,256,128]{4,3,2,1,0:T(8,128)(2,1)}, f32[27,128,128]{2,1,0:T(8,128)}, f32[27,128,128]{2,1,0:T(8,128)}) custom-call(bf16[2,2,4,256,128]{4,3,2,1,0:T(8,128)(2,1)S(1)} %get-tuple-element.12.y_vm, bf16[2,2,4,256,128]{4,3,2,1,0:T(8,128)(2,1)S(1)} %get-tuple-element.13.dx_vm, ...), custom_call_target="tpu_custom_call" | custom-call | tf_op jit(solution)/shard_map/pallas_call | solution.py:642

commit v3 on v1

--- a/solution.py
+++ b/solution.py
@@ -18,14 +18,17 @@
 RING = 4
 TAPS = 28
 TQ = TAPS // RING
+OFFS = (1, 2, 3)
+TAIL, TAIL_ORDER = 18, (0, 2, 1)
+FAR_FIRST = (2, 1, 3)
 
 
 def kernel(width, depth_count,
            x_hbm, w1_hbm, w2_hbm, g_hbm,
            y_out, dx_out, dw1_out, dw2_out,
            xe, ge, ze, ae, w1, w2, acc1, acc2, dgel, zt, at,
-           p2, p1, cr, ra, rb, rl, rr, bz, r2, xb, ds,
-           hs_send, hs_recv, rs_send, rs_recv, ar_send, ar_recv, lsem):
+           p2, p1, cr, ra, rb, rl, rr, bz, r2, xb, ds, hold,
+           hs_send, hs_recv, rs_send, rs_recv, ar_send, ar_recv, hold_send, hold_recv, lsem):
     rows = NH * width
     row = lax.axis_index("row")
     dep = lax.axis_index("dep")
@@ -49,85 +52,101 @@
 
     has_below = dep > 0
     has_above = dep < depth_count - 1
-
-    def face(k, src_of, up, part):
-        h0, hn = (edge, 1) if part == 0 else (row, NH - 1)
-        d_src, d_dst = (ND - 1, 0) if up else (0, ND + 1)
-        dev = (row, dep + 1) if up else (row, dep - 1)
-        n = 2 * part + (0 if up else 1)
-        return rdma(src_of(d_src, h0, hn), exts[k].at[:, d_dst, pl.ds(1 + h0, hn)], hs_send.at[k, n], hs_recv.at[k, n], dev)
-
-    def side(k, src_of):
-        return rdma(src_of(None, edge, 1), exts[k].at[:, pl.ds(1, ND), pl.ds(my_pad, 1)], rs_send.at[k, 0], rs_recv.at[k, 0], (other, dep))
+    near_above, near_below = x < RING - 1, x > 0
+
+    lines_out = (edge, row, row + 1, row + 2)
+    ways = ((True, has_above, has_below, near_above), (False, has_below, has_above, near_below))
+    hops = {2: (2, 3), 3: (1, 3)}
+
+    def source(k, up, n):
+        d = ND - 1 if up else 0
+        if k < 2:
+            return (x_hbm, g_hbm)[k].at[:, d, pl.ds(lines_out[n], 1)]
+        return exts[k].at[:, d + 1, pl.ds(1 + lines_out[n], 1)]
+
+    def landing(k, up, n):
+        return exts[k].at[:, 0 if up else ND + 1, pl.ds(1 + lines_out[n], 1)]
+
+    def face(k, up, n):
+        slot = 2 * n + up
+        return rdma(source(k, up, n), landing(k, up, n), hs_send.at[k, slot], hs_recv.at[k, slot], (row, dep + (2 * up - 1)))
+
+    def far_hop(k, up, n):
+        i = hops[k].index(n)
+        return rdma(source(k, up, n), hold.at[k - 2, i], hold_send.at[k - 2, i], hold_recv.at[k - 2, i], (row, dep + RING * (2 * up - 1)))
+
+    def far_land(k, up, n):
+        i = hops[k].index(n)
+        return rdma(hold.at[k - 2, i], landing(k, up, n), hold_send.at[k - 2, 2 + i], hs_recv.at[k, 2 * n + up], (row, dep - (RING - 1) * (2 * up - 1)))
+
+    def side(k):
+        if k < 2:
+            src = (x_hbm, g_hbm)[k].at[:, :, pl.ds(edge, 1)]
+        else:
+            src = exts[k].at[:, pl.ds(1, ND), pl.ds(1 + edge, 1)]
+        return rdma(src, exts[k].at[:, pl.ds(1, ND), pl.ds(my_pad, 1)], rs_send.at[k, 0], rs_recv.at[k, 0], (other, dep))
 
     def corner(k, up):
-        d_dst = 0 if up else ND + 1
-        n = 1 if up else 2
-        return rdma(exts[k].at[:, d_dst, pl.ds(1 + edge, 1)], exts[k].at[:, d_dst, pl.ds(my_pad, 1)], rs_send.at[k, n], rs_recv.at[k, n], (other, dep))
-
-    def from_hbm(ref):
-        def src(d, h0, hn):
-            return ref.at[:, pl.ds(0, ND) if d is None else d, pl.ds(h0, hn)]
-        return src
-
-    def from_ext(ref):
-        def src(d, h0, hn):
-            return ref.at[:, pl.ds(1, ND) if d is None else 1 + d, pl.ds(1 + h0, hn)]
-        return src
-
-    sources = (from_hbm(x_hbm), from_hbm(g_hbm), from_ext(ze), from_ext(ae))
-
-    def send_faces(k):
-        side(k, sources[k]).start()
-        for part in range(2):
-            @pl.when(has_above)
+        at_face = exts[k].at[:, 0 if up else ND + 1]
+        return rdma(at_face.at[:, pl.ds(1 + edge, 1)], at_face.at[:, pl.ds(my_pad, 1)], rs_send.at[k, 1 + up], rs_recv.at[k, 1 + up], (other, dep))
+
+    relays = ((x == RING - 1) & (dep >= RING), (x == 0) & (dep < depth_count - RING))
+
+    def each_face(k, do, which):
+        for n in which:
+            far_way = n in hops.get(k, ())
+            for up, has, _, near in ways:
+                @pl.when(near if far_way else has)
+                def _():
+                    do(face(k, up, n))
+
+                if far_way:
+                    @pl.when(has & jnp.logical_not(near))
+                    def _():
+                        do(far_hop(k, up, n))
+
+    def start(copy):
+        copy.start()
+
+    def sent(copy):
+        copy.wait_send()
+
+    def relay_far(k, which):
+        for (up, *_), cond in zip(ways, relays):
+            @pl.when(cond)
             def _():
-                face(k, sources[k], True, part).start()
-
-            @pl.when(has_below)
+                for n in which:
+                    far_hop(k, up, n).wait_recv()
+                    far_land(k, up, n).start()
+
+    def pass_corners(k):
+        for up, _, comes, *_ in ways:
+            @pl.when(comes)
             def _():
-                face(k, sources[k], False, part).start()
-
-    def pass_corners(k):
-        @pl.when(has_below)
-        def _():
-            face(k, sources[k], True, 0).wait_recv()
-            corner(k, True).start()
-
-        @pl.when(has_above)
-        def _():
-            face(k, sources[k], False, 0).wait_recv()
-            corner(k, False).start()
+                face(k, up, 0).wait_recv()
+                corner(k, up).start()
 
     def take_faces(k):
-        @pl.when(has_below)
-        def _():
-            face(k, sources[k], True, 1).wait_recv()
-            corner(k, True).wait_recv()
-
-        @pl.when(has_above)
-        def _():
-            face(k, sources[k], False, 1).wait_recv()
-            corner(k, False).wait_recv()
+        for up, _, comes, *_ in ways:
+            @pl.when(comes)
+            def _():
+                corner(k, up).wait_recv()
+                for n in OFFS:
+                    face(k, up, n).wait_recv()
 
     def finish_halo(k):
-        side(k, sources[k]).wait_send()
-        for part in range(2):
-            @pl.when(has_above)
+        side(k).wait_send()
+        each_face(k, sent, range(NH))
+        for (up, *_), cond in zip(ways, relays):
+            @pl.when(cond)
             def _():
-                face(k, sources[k], True, part).wait_send()
-
-            @pl.when(has_below)
+                for n in hops.get(k, ()):
+                    far_land(k, up, n).wait_send()
+
+        for up, _, comes, *_ in ways:
+            @pl.when(comes)
             def _():
-                face(k, sources[k], False, part).wait_send()
-
-        @pl.when(has_below)
-        def _():
-            corner(k, True).wait_send()
-
-        @pl.when(has_above)
-        def _():
-            corner(k, False).wait_send()
+                corner(k, up).wait_send()
 
     barrier = pltpu.get_barrier_semaphore()
     pl.semaphore_signal(barrier, inc=1, device_id=(other, dep), device_id_type=MESH)
@@ -135,7 +154,7 @@
         for off in range(1, RING):
             pl.semaphore_signal(barrier, inc=1, device_id=(row, ring_dep(axis, off)), device_id_type=MESH)
 
-    for step in (1, depth_count - 1):
+    for step in (1, depth_count - 1, RING, depth_count - RING):
         pl.semaphore_signal(barrier, inc=1, device_id=(row, lax.rem(dep + step, depth_count)), device_id_type=MESH)
 
     loads = [
@@ -147,10 +166,11 @@
     for load in loads:
         load.start()
 
-    pl.semaphore_wait(barrier, 12)
-
-    send_faces(0)
-    send_faces(1)
+    pl.semaphore_wait(barrier, 14)
+
+    for k in range(2):
+        side(k).start()
+        each_face(k, start, range(NH))
 
     zero_row = jnp.zeros((NB, 1, width, NC), BF16)
     for ext in exts:
@@ -189,7 +209,7 @@
     def mul(lhs, rhs, flip):
         return lax.dot_general(lhs, rhs, (((1,), (1 if flip else 0,)), ((), ())), preferred_element_type=F32)
 
-    def conv_inner(ext, w, acc, flip):
+    def conv_inner(ext, w, acc, flip, b0=0, b1=NB):
         cells = []
         for dd in (1, 2):
             for th in range(3):
@@ -205,7 +225,7 @@
                     acc[b, d * 3 + tw] = out[:, j * NC:(j + 1) * NC]
             return carry
 
-        lax.fori_loop(0, NB, one, 0)
+        lax.fori_loop(b0, b1, one, 0)
 
     def conv_outer(ext, w, acc, flip):
         def one(i, carry):
@@ -228,14 +248,15 @@
         return jnp.where(wpos < width - 1, pltpu.roll(v, width - 1, 0), 0.0)
 
     def each_row(acc, use):
-        def one(i, carry):
-            b, d, h = i // (ND * NH), lax.rem(i // NH, ND), lax.rem(i, NH)
-            at_rows = pl.ds(pl.multiple_of(h * width, width), width)
-            total = acc[b, d * 3 + 1, at_rows] + from_left(acc[b, d * 3, at_rows]) + from_right(acc[b, d * 3 + 2, at_rows])
-            use(i, b, d, h, total)
+        def one(j, carry):
+            for i in (2 * j, 2 * j + 1):
+                b, d, h = i // (ND * NH), lax.rem(i // NH, ND), lax.rem(i, NH)
+                at_rows = pl.ds(pl.multiple_of(h * width, width), width)
+                total = acc[b, d * 3 + 1, at_rows] + from_left(acc[b, d * 3, at_rows]) + from_right(acc[b, d * 3 + 2, at_rows])
+                use(i, b, d, h, total)
             return carry
 
-        lax.fori_loop(0, NB * ND * NH, one, 0)
+        lax.fori_loop(0, NB * ND * NH // 2, one, 0)
 
     def after_conv1(i, b, d, h, total):
         a = total.astype(BF16).astype(F32)
@@ -260,24 +281,29 @@
         return use
 
     def tap_index(td, th):
-        return td * 6 + th * 3 if th < 2 else 18 + td * 3
-
-    def weight_grad(own_t, ext, part, swap, between):
+        return td * 6 + th * 3 if th < 2 else TAIL + 3 * TAIL_ORDER.index(td)
+
+    def weight_grad(own_t, ext, part, swap, which, between):
         def rhs(td, th):
             d0, h0 = (2 - td, 2 - th) if swap else (td, th)
             return jnp.concatenate([lines(ext, b, d + d0, h0) for b in range(NB) for d in range(ND)], axis=0)
 
         def product(right):
-            lhs = jnp.concatenate([own_t[i] for i in range(NB * ND * NH)], axis=1)
-            return jnp.dot(lhs, right, preferred_element_type=F32)
+            cut = 3 * NC // 2
+            halves = []
+            for top in (0, cut):
+                lhs = jnp.concatenate([own_t[i, pl.ds(top, cut)] for i in range(NB * ND * NH)], axis=1)
+                halves.append(jnp.dot(lhs, right, preferred_element_type=F32))
+            return jnp.concatenate(halves, axis=0)
 
         def put(out, n, td, th):
             for tw in range(3):
                 blk = out[tw * NC:(tw + 1) * NC, n * NC:(n + 1) * NC]
                 part[tap_index(td, th) + tw] = blk if swap else blk.T
 
-        groups = [((td, 0), (td, 1)) for td in range(3)] + [((0, 2), (1, 2)), ((2, 2),)]
-        for k, taps in enumerate(groups):
+        groups = [((td, 0), (td, 1)) for td in range(3)] + [((0, 2), (2, 2)), ((1, 2),)]
+        for k in which:
+            taps = groups[k]
             out = product(jnp.concatenate([rhs(*t) for t in taps], axis=1))
             for n, t in enumerate(taps):
                 put(out, n, *t)
@@ -303,8 +329,8 @@
 
     def pair_copy(s, n):
         theirs = pl.ds(pl.multiple_of(other * half, half), half)
-        taps = pl.ds(0, 18) if n == 0 else pl.ds(18, TAPS - 18)
-        return rdma(parts[s].at[taps, theirs], cr.at[s, taps], *sems(2 * s + n, 22), (other, dep))
+        taps = (pl.ds(0, TAIL), pl.ds(TAIL, 6), pl.ds(TAIL + 6, 4))[n]
+        return rdma(parts[s].at[taps, theirs], cr.at[s, taps], *sems(s, 26 + n), (other, dep))
 
     def scatter_copy(q, n):
         part = parts[q // 2]
@@ -344,15 +370,21 @@
         src = ds.at[q, taps] if n < 4 else out.at[taps, chunk(q, off)]
         return rdma(src, out.at[taps, chunk(q, off)], *sems(q, 15 + n), dev)
 
-    def last_copy(q):
-        rows_q = pl.ds(pl.multiple_of(row * half + (q % 2) * (half // 2), half // 2), half // 2)
-        return rdma(outs[q // 2].at[:, rows_q], outs[q // 2].at[:, rows_q], *sems(q, 21), (other, dep))
+    def out_copy(q, n):
+        out = outs[q // 2]
+        taps, off = ((pl.ds(0, 27), 0), (pl.ds(0, 27), 3), (pl.ds(0, 27), 1), (low, 2), (high27, 2))[n]
+        src = ds.at[q, taps] if n == 0 else out.at[taps, chunk(q, off)]
+        return rdma(src, out.at[taps, chunk(q, off)], *sems(q, 21 + n), (other, dep))
 
     my_half = pl.ds(pl.multiple_of(row * half, half), half)
 
+    def both(step, q):
+        step(q)
+        step(q + 1)
+
     def step_pair(s):
-        pair_copy(s, 0).wait_recv()
-        pair_copy(s, 1).wait_recv()
+        for n in range(3):
+            pair_copy(s, n).wait_recv()
 
         def add(t, carry):
             parts[s][t, my_half] += cr[s, t]
@@ -377,31 +409,32 @@
         for n in range(2, 6):
             scatter_copy(q, n).wait_recv()
         bz[q] = parts[q // 2][:, chunk(q, 0)] + (rl[q] + rr[q])
-        for off in (2, 1, 3):
+        for off in FAR_FIRST:
             second_copy(q, off).start()
 
     def step_second(q):
-        for off in (1, 2, 3):
+        for off in OFFS:
             second_copy(q, off).wait_recv()
         c = coord[axes[q % 2][1]]
         xb[q, x] = (bz[q, pl.ds(c * TQ, TQ)] + r2[q, 0]) + (r2[q, 1] + r2[q, 2])
-        for off in (2, 1, 3):
+        for off in FAR_FIRST:
             third_copy(q, off, x).start()
 
     def step_third(q):
-        for off in (1, 2, 3):
+        for off in OFFS:
             third_copy(q, off, turn(x, RING - off)).wait_recv()
         c = coord[axes[q % 2][1]]
         ds[q, pl.ds(c * TQ, TQ)] = (xb[q, 0] + xb[q, 1]) + (xb[q, 2] + xb[q, 3])
-        for off in (2, 1, 3):
+        for off in FAR_FIRST:
             fourth_copy(q, off, c).start()
 
     def step_fourth(q):
         c = coord[axes[q % 2][1]]
-        for off in (1, 2, 3):
+        for off in OFFS:
             fourth_copy(q, off, turn(c, RING - off)).wait_recv()
         for n in range(4):
             gather_copy(q, n).start()
+        out_copy(q, 0).start()
         outs[q // 2][:, chunk(q, 0)] = ds[q, pl.ds(0, 27)]
 
     def step_forward(q):
@@ -413,15 +446,15 @@
     def step_fifth(q):
         for n in range(2, 6):
             gather_copy(q, n).wait_recv()
-        last_copy(q).start()
+            out_copy(q, n - 1).start()
 
     def finish_sum(q):
-        last_copy(q).wait()
-        pair_copy(q // 2, q % 2).wait_send()
+        for n in range(5):
+            out_copy(q, n).wait()
         for n in range(6):
             scatter_copy(q, n).wait_send()
             gather_copy(q, n).wait_send()
-        for off in (1, 2, 3):
+        for off in OFFS:
             second_copy(q, off).wait_send()
             third_copy(q, off, x).wait_send()
             fourth_copy(q, off, coord[axes[q % 2][1]]).wait_send()
@@ -429,82 +462,78 @@
     def after_dw2(k):
         if k == 2:
             pair_copy(0, 0).start()
-        if k == 4:
+        if k == 3:
             pair_copy(0, 1).start()
+            pair_copy(0, 2).start()
 
     def after_dw1(k):
-        if k == 1:
-            step_relay(0)
-            step_relay(1)
+        if k >= 2:
+            pair_copy(1, k - 2).start()
         if k == 2:
-            pair_copy(1, 0).start()
-        if k == 4:
-            pair_copy(1, 1).start()
+            both(step_relay, 0)
 
     loads[0].wait()
     loads[1].wait()
-    side(0, sources[0]).wait_recv()
+    side(0).wait_recv()
     conv_inner(xe, w1, acc1, False)
     loads[2].wait()
     loads[3].wait()
-    side(1, sources[1]).wait_recv()
+    side(1).wait_recv()
     conv_inner(ge, w2, acc2, True)
     pass_corners(0)
     take_faces(0)
     conv_outer(xe, w1, acc1, False)
     each_row(acc1, after_conv1)
-    send_faces(2)
+    side(2).start()
+    each_face(2, start, range(NH))
     pass_corners(1)
-    side(2, sources[2]).wait_recv()
+    side(2).wait_recv()
     conv_inner(ze, w2, acc1, False)
+    weight_grad(zt, ge, p2, True, (1, 4), after_dw2)
     take_faces(1)
-    weight_grad(zt, ge, p2, True, after_dw2)
+    weight_grad(zt, ge, p2, True, (0, 2, 3), after_dw2)
+    relay_far(2, hops[2])
     conv_outer(ge, w2, acc2, True)
     step_pair(0)
     each_row(acc2, after_conv_g)
-    send_faces(3)
-    weight_grad(at, xe, p1, False, after_dw1)
+    side(3).start()
+    each_face(3, start, range(2))
+    weight_grad(at, xe, p1, False, range(5), after_dw1)
     pass_corners(2)
-    step_first(0)
-    step_first(1)
     step_pair(1)
+    relay_far(3, (1,))
+    both(step_first, 0)
     take_faces(2)
     conv_outer(ze, w2, acc1, False)
-    step_second(0)
-    step_second(1)
+    both(step_relay, 2)
+    side(3).wait_recv()
+    conv_inner(ae, w1, acc2, True, 0, 1)
+    both(step_second, 0)
+    each_face(3, start, (2, 3))
     each_row(acc1, after_add(xe, y_out))
-    step_relay(2)
-    step_relay(3)
-    side(3, sources[3]).wait_recv()
-    conv_inner(ae, w1, acc2, True)
-    step_third(0)
-    step_third(1)
-    step_first(2)
-    step_first(3)
+    both(step_first, 2)
+    both(step_third, 0)
     pass_corners(3)
+    conv_inner(ae, w1, acc2, True, 1, 2)
+    both(step_second, 2)
+    relay_far(3, (3,))
+    both(step_fourth, 0)
+    both(step_third, 2)
+    both(step_forward, 0)
+    both(step_fourth, 2)
     take_faces(3)
     conv_outer(ae, w1, acc2, True)
     each_row(acc2, after_add(ge, dx_out))
-    step_fourth(0)
-    step_fourth(1)
-    step_second(2)
-    step_second(3)
-    step_forward(0)
-    step_forward(1)
-    step_third(2)
-    step_third(3)
-    step_fifth(0)
-    step_fifth(1)
-    step_fourth(2)
-    step_fourth(3)
-    step_forward(2)
-    step_forward(3)
-    step_fifth(2)
-    step_fifth(3)
+    both(step_forward, 2)
+    both(step_fifth, 0)
+    both(step_fifth, 2)
     for k in range(4):
         finish_halo(k)
     for q in range(4):
         finish_sum(q)
+    for s in range(2):
+        for n in range(3):
+            pair_copy(s, n).wait_send()
 
 
 def to_hbm(y_vm, dx_vm, dw1_vm, dw2_vm, y_hbm, dx_hbm, dw1_hbm, dw2_hbm, sem):
@@ -512,7 +541,7 @@
     for src, dst in ((dw1_vm, dw1_hbm), (dw2_vm, dw2_hbm)):
         for td in range(3):
             copies.append((src.at[pl.ds(td * 6, 6)], dst.at[pl.ds(td * 9, 6)]))
-            copies.append((src.at[pl.ds(18 + td * 3, 3)], dst.at[pl.ds(td * 9 + 6, 3)]))
+            copies.append((src.at[pl.ds(TAIL + 3 * TAIL_ORDER.index(td), 3)], dst.at[pl.ds(td * 9 + 6, 3)]))
     started = [pltpu.make_async_copy(src, dst, sem.at[n]) for n, (src, dst) in enumerate(copies)]
     for copy in started:
         copy.start()
@@ -556,12 +585,15 @@
                 pltpu.VMEM((4, RING - 1, TQ, NC // 16, NC), F32),
                 pltpu.VMEM((4, RING, TQ, NC // 16, NC), F32),
                 pltpu.VMEM((4, TAPS, NC // 16, NC), F32),
-                pltpu.SemaphoreType.DMA((4, 4)),
-                pltpu.SemaphoreType.DMA((4, 4)),
+                pltpu.VMEM((2, 2, NB, 1, width, NC), BF16),
+                pltpu.SemaphoreType.DMA((4, 8)),
+                pltpu.SemaphoreType.DMA((4, 8)),
                 pltpu.SemaphoreType.DMA((4, 3)),
                 pltpu.SemaphoreType.DMA((4, 3)),
-                pltpu.SemaphoreType.DMA((4, 23)),
-                pltpu.SemaphoreType.DMA((4, 23)),
+                pltpu.SemaphoreType.DMA((4, 29)),
+                pltpu.SemaphoreType.DMA((4, 29)),
+                pltpu.SemaphoreType.DMA((2, 4)),
+                pltpu.SemaphoreType.DMA((2, 2)),
                 pltpu.SemaphoreType.DMA((4,)),
             ],
             compiler_params=pltpu.CompilerParams(collective_id=0, has_side_effects=True, vmem_limit_bytes=56 * 1000 * 1000),

time: 97.9 us -> 87.5 us (0.89)
  Pallas kernels: 97 us -> 86.6 us
    pallas_call x1, Pallas kernels: 94.5 us -> 84 us  [local_step(): pl.pallas_call(functools.partial(kernel, width, depth_count), out_shape=(...]
where the time goes in v3:
time: 87.5 us; the launch traced here: 87.4 us
  Pallas kernels  86.6 us (99%)
    pallas_call x1, Pallas kernels, local_step(): pl.pallas_call(functools.partial(kernel, width, depth_count), out_shape=(...  84 us
    pallas_call x1, Pallas kernels, local_step(): pl.pallas_call(to_hbm, out_shape=(jax.ShapeDtypeStruct(x_tile.shape, BF16...  2.56 us

profile of v3, /device:TPU:1, one launch (start us, length us, event | category | flops | bytes accessed | tf_op | source)
XLA Modules:
  0.0 87.4 jit_solution(6912468443868720229)
XLA Ops:
  0.6 84.0 %shard_map.75 = (bf16[2,2,4,256,128]{4,3,2,1,0:T(8,128)(2,1)S(1)}, bf16[2,2,4,256,128]{4,3,2,1,0:T(8,128)(2,1)S(1)}, f32[27,128,128]{2,1,0:T(8,128)S(1)}, f32[27,128,128]{2,1,0:T(8,128)S(1)}) custom-call(bf16[2,2,4,256,128]{4,3,2,1,0:T(8,128)(2,1)} %x_hbm.1, bf16[3,3,3,128,128]{4,3,2,1,0:T(8,128)(2,1)} %w1_hbm.1, bf16[3,3,3,128,128]{4,3,2,1,0:T(8,128)(2,1)} %w2_hbm.1, ...), custom_call_target="tpu_custom_call" | custom-call | tf_op jit(solution)/shard_map/pallas_call | solution.py:564
  84.7 2.6 %shard_map.76 = (bf16[2,2,4,256,128]{4,3,2,1,0:T(8,128)(2,1)}, bf16[2,2,4,256,128]{4,3,2,1,0:T(8,128)(2,1)}, f32[27,128,128]{2,1,0:T(8,128)}, f32[27,128,128]{2,1,0:T(8,128)}) custom-call(bf16[2,2,4,256,128]{4,3,2,1,0:T(8,128)(2,1)S(1)} %get-tuple-element.12.y_vm, bf16[2,2,4,256,128]{4,3,2,1,0:T(8,128)(2,1)S(1)} %get-tuple-element.13.dx_vm, ...), custom_call_target="tpu_custom_call" | custom-call | tf_op jit(solution)/shard_map/pallas_call | solution.py:601

commit v4 on v3

--- a/solution.py
+++ b/solution.py
@@ -18,7 +18,6 @@
 RING = 4
 TAPS = 28
 TQ = TAPS // RING
-OFFS = (1, 2, 3)
 TAIL, TAIL_ORDER = 18, (0, 2, 1)
 FAR_FIRST = (2, 1, 3)
 
@@ -27,7 +26,7 @@
            x_hbm, w1_hbm, w2_hbm, g_hbm,
            y_out, dx_out, dw1_out, dw2_out,
            xe, ge, ze, ae, w1, w2, acc1, acc2, dgel, zt, at,
-           p2, p1, cr, ra, rb, rl, rr, bz, r2, xb, ds, hold,
+           p2, p1, cr, ra, rb, lr, bz, r2, xb, ds, hold,
            hs_send, hs_recv, rs_send, rs_recv, ar_send, ar_recv, hold_send, hold_recv, lsem):
     rows = NH * width
     row = lax.axis_index("row")
@@ -57,6 +56,7 @@
     lines_out = (edge, row, row + 1, row + 2)
     ways = ((True, has_above, has_below, near_above), (False, has_below, has_above, near_below))
     hops = {2: (2, 3), 3: (1, 3)}
+    every, early, late = range(NH), range(2), range(2, NH)
 
     def source(k, up, n):
         d = ND - 1 if up else 0
@@ -68,8 +68,11 @@
         return exts[k].at[:, 0 if up else ND + 1, pl.ds(1 + lines_out[n], 1)]
 
     def face(k, up, n):
-        slot = 2 * n + up
-        return rdma(source(k, up, n), landing(k, up, n), hs_send.at[k, slot], hs_recv.at[k, slot], (row, dep + (2 * up - 1)))
+        return rdma(source(k, up, n), landing(k, up, n), hs_send.at[k, int(up)], hs_recv.at[k, int(up), min(n, 1)], (row, dep + (2 * up - 1)))
+
+    def rows_of(k, up, count):
+        ref = exts[k].at[:, 0, pl.ds(1, count)]
+        return rdma(ref, ref, hs_send.at[k, int(up)], hs_recv.at[k, int(up), 1], (row, dep))
 
     def far_hop(k, up, n):
         i = hops[k].index(n)
@@ -77,7 +80,7 @@
 
     def far_land(k, up, n):
         i = hops[k].index(n)
-        return rdma(hold.at[k - 2, i], landing(k, up, n), hold_send.at[k - 2, 2 + i], hs_recv.at[k, 2 * n + up], (row, dep - (RING - 1) * (2 * up - 1)))
+        return rdma(hold.at[k - 2, i], landing(k, up, n), hold_send.at[k - 2, 2 + i], hs_recv.at[k, int(up), 1], (row, dep - (RING - 1) * (2 * up - 1)))
 
     def side(k):
         if k < 2:
@@ -92,24 +95,21 @@
 
     relays = ((x == RING - 1) & (dep >= RING), (x == 0) & (dep < depth_count - RING))
 
-    def each_face(k, do, which):
-        for n in which:
-            far_way = n in hops.get(k, ())
+    def each_face(k, do, which, far_which):
+        for n in range(NH):
             for up, has, _, near in ways:
-                @pl.when(near if far_way else has)
-                def _():
-                    do(face(k, up, n))
-
-                if far_way:
+                if n in which:
+                    @pl.when(near)
+                    def _():
+                        do(face(k, up, n))
+
+                if n in far_which:
                     @pl.when(has & jnp.logical_not(near))
                     def _():
-                        do(far_hop(k, up, n))
+                        do((far_hop if n in hops.get(k, ()) else face)(k, up, n))
 
     def start(copy):
         copy.start()
-
-    def sent(copy):
-        copy.wait_send()
 
     def relay_far(k, which):
         for (up, *_), cond in zip(ways, relays):
@@ -131,12 +131,21 @@
             @pl.when(comes)
             def _():
                 corner(k, up).wait_recv()
-                for n in OFFS:
-                    face(k, up, n).wait_recv()
+                rows_of(k, up, NH - 1).wait_recv()
 
     def finish_halo(k):
         side(k).wait_send()
-        each_face(k, sent, range(NH))
+        for up, has, _, near in ways:
+            @pl.when(near)
+            def _():
+                rows_of(k, up, NH).wait_send()
+
+            @pl.when(has & jnp.logical_not(near))
+            def _():
+                rows_of(k, up, NH - len(hops.get(k, ()))).wait_send()
+                for n in hops.get(k, ()):
+                    far_hop(k, up, n).wait_send()
+
         for (up, *_), cond in zip(ways, relays):
             @pl.when(cond)
             def _():
@@ -170,7 +179,7 @@
 
     for k in range(2):
         side(k).start()
-        each_face(k, start, range(NH))
+        each_face(k, start, every, every)
 
     zero_row = jnp.zeros((NB, 1, width, NC), BF16)
     for ext in exts:
@@ -210,11 +219,8 @@
         return lax.dot_general(lhs, rhs, (((1,), (1 if flip else 0,)), ((), ())), preferred_element_type=F32)
 
     def conv_inner(ext, w, acc, flip, b0=0, b1=NB):
-        cells = []
-        for dd in (1, 2):
-            for th in range(3):
-                cells.append([(dd, th, 0), (dd, th, 1), (dd - 1, th, 0), (dd - 1, th, 1), (dd, th, 2), (dd - 1, th, 2)])
         order = ((0, 0), (0, 1), (1, 0), (1, 1), (0, 2), (1, 2))
+        cells = [[(dd - d, th, tw) for d, tw in order] for dd in (1, 2) for th in range(3)]
 
         def one(b, carry):
             lhs = jnp.concatenate([lines(ext, b, dd, th) for dd in (1, 2) for th in range(3)], axis=1)
@@ -227,14 +233,15 @@
 
         lax.fori_loop(b0, b1, one, 0)
 
+    def outer_block(ext, w, acc, flip, b, d):
+        lhs = jnp.concatenate([lines(ext, b, 3 * d, th) for th in range(3)], axis=1)
+        out = mul(lhs, weights(w, [[(2 * d, th, tw) for tw in range(3)] for th in range(3)], flip), flip)
+        for tw in range(3):
+            acc[b, d * 3 + tw] += out[:, tw * NC:(tw + 1) * NC]
+
     def conv_outer(ext, w, acc, flip):
         def one(i, carry):
-            b, d = i // ND, lax.rem(i, ND)
-            td = 2 * d
-            lhs = jnp.concatenate([lines(ext, b, 3 * d, th) for th in range(3)], axis=1)
-            out = mul(lhs, weights(w, [[(td, th, tw) for tw in range(3)] for th in range(3)], flip), flip)
-            for tw in range(3):
-                acc[b, d * 3 + tw] += out[:, tw * NC:(tw + 1) * NC]
+            outer_block(ext, w, acc, flip, i // ND, lax.rem(i, ND))
             return carry
 
         lax.fori_loop(0, NB * ND, one, 0)
@@ -247,16 +254,27 @@
     def from_right(v):
         return jnp.where(wpos < width - 1, pltpu.roll(v, width - 1, 0), 0.0)
 
+    def one_row(acc, use, b, d, h):
+        at_rows = pl.ds(h * width, width)
+        total = acc[b, d * 3 + 1, at_rows] + from_left(acc[b, d * 3, at_rows]) + from_right(acc[b, d * 3 + 2, at_rows])
+        use((b * ND + d) * NH + h, b, d, h, total)
+
     def each_row(acc, use):
         def one(j, carry):
-            for i in (2 * j, 2 * j + 1):
-                b, d, h = i // (ND * NH), lax.rem(i // NH, ND), lax.rem(i, NH)
-                at_rows = pl.ds(pl.multiple_of(h * width, width), width)
-                total = acc[b, d * 3 + 1, at_rows] + from_left(acc[b, d * 3, at_rows]) + from_right(acc[b, d * 3 + 2, at_rows])
-                use(i, b, d, h, total)
+            for h in range(NH):
+                one_row(acc, use, j // ND, lax.rem(j, ND), h)
             return carry
 
-        lax.fori_loop(0, NB * ND * NH // 2, one, 0)
+        lax.fori_loop(0, NB * ND, one, 0)
+
+    def conv_outer_rows(ext, w, acc, flip, use):
+        blocks = [(b, d) for b in range(NB) for d in range(ND)]
+        for now, done in zip(blocks + [()], [()] + blocks):
+            if now:
+                outer_block(ext, w, acc, flip, *now)
+            if done:
+                for h in range(NH):
+                    one_row(acc, use, *done, h)
 
     def after_conv1(i, b, d, h, total):
         a = total.astype(BF16).astype(F32)
@@ -330,7 +348,7 @@
     def pair_copy(s, n):
         theirs = pl.ds(pl.multiple_of(other * half, half), half)
         taps = (pl.ds(0, TAIL), pl.ds(TAIL, 6), pl.ds(TAIL + 6, 4))[n]
-        return rdma(parts[s].at[taps, theirs], cr.at[s, taps], *sems(s, 26 + n), (other, dep))
+        return rdma(parts[s].at[taps, theirs], cr.at[s, taps], *sems(s, 10), (other, dep))
 
     def scatter_copy(q, n):
         part = parts[q // 2]
@@ -338,23 +356,23 @@
         src, dst, dev = (
             (part.at[low, chunk(q, 2)], ra.at[q], nxt),
             (part.at[high, chunk(q, 2)], rb.at[q], prv),
-            (part.at[high, chunk(q, 1)], rl.at[q, high], nxt),
-            (part.at[low, chunk(q, 3)], rr.at[q, low], prv),
-            (ra.at[q], rl.at[q, low], nxt),
-            (rb.at[q], rr.at[q, high], prv),
+            (part.at[high, chunk(q, 1)], lr.at[q, 0, high], nxt),
+            (part.at[low, chunk(q, 3)], lr.at[q, 1, low], prv),
+            (ra.at[q], lr.at[q, 0, low], nxt),
+            (rb.at[q], lr.at[q, 1, high], prv),
         )[n]
-        return rdma(src, dst, *sems(q, n), dev)
+        return rdma(src, dst, *sems(q, min(n, 2)), dev)
 
     def second_copy(q, off):
         axis = axes[q % 2][1]
         j = turn(coord[axis], off)
-        return rdma(bz.at[q, pl.ds(j * TQ, TQ)], r2.at[q, off - 1], *sems(q, 5 + off), (row, ring_dep(axis, off)))
+        return rdma(bz.at[q, pl.ds(j * TQ, TQ)], r2.at[q, off - 1], *sems(q, 3), (row, ring_dep(axis, off)))
 
     def third_copy(q, off, slot):
-        return rdma(xb.at[q, slot], xb.at[q, slot], *sems(q, 8 + off), (row, ring_dep("x", off)))
+        return rdma(xb.at[q, slot], xb.at[q, slot], *sems(q, 4), (row, ring_dep("x", off)))
 
     def fourth_copy(q, off, j):
-        return rdma(ds.at[q, pl.ds(j * TQ, TQ)], ds.at[q, pl.ds(j * TQ, TQ)], *sems(q, 11 + off), (row, ring_dep(axes[q % 2][1], off)))
+        return rdma(ds.at[q, pl.ds(j * TQ, TQ)], ds.at[q, pl.ds(j * TQ, TQ)], *sems(q, 5), (row, ring_dep(axes[q % 2][1], off)))
 
     def gather_copy(q, n):
         out = outs[q // 2]
@@ -368,23 +386,32 @@
             (high27, 1, prv),
         )[n]
         src = ds.at[q, taps] if n < 4 else out.at[taps, chunk(q, off)]
-        return rdma(src, out.at[taps, chunk(q, off)], *sems(q, 15 + n), dev)
+        return rdma(src, out.at[taps, chunk(q, off)], *sems(q, 6 + min(n, 2)), dev)
 
     def out_copy(q, n):
         out = outs[q // 2]
-        taps, off = ((pl.ds(0, 27), 0), (pl.ds(0, 27), 3), (pl.ds(0, 27), 1), (low, 2), (high27, 2))[n]
-        src = ds.at[q, taps] if n == 0 else out.at[taps, chunk(q, off)]
-        return rdma(src, out.at[taps, chunk(q, off)], *sems(q, 21 + n), (other, dep))
+        taps, off = ((low, 3), (high27, 1), (high27, 3), (low, 1), (low, 2), (high27, 2), (pl.ds(0, 27), 0))[n]
+        src = ds.at[q, taps] if off == 0 else out.at[taps, chunk(q, off)]
+        return rdma(src, out.at[taps, chunk(q, off)], *sems(q, 9), (other, dep))
+
+    def group(q, n):
+        ref = {
+            0: ra.at[q], 1: rb.at[q], 2: lr.at[q], 3: r2.at[q], 4: r2.at[q], 5: r2.at[q],
+            6: ra.at[q], 7: ra.at[q, pl.ds(1, TAPS // 2 - 1)],
+            8: outs[0].at[:, pl.ds(0, 2 * piece)], 9: outs[0].at[:, pl.ds(0, 4 * piece)], 10: cr.at[0],
+        }[n]
+        return rdma(ref, ref, *sems(q, n), (other, dep))
 
     my_half = pl.ds(pl.multiple_of(row * half, half), half)
+
+    dw2_q, dw1_q = 0, 2
 
     def both(step, q):
         step(q)
         step(q + 1)
 
     def step_pair(s):
-        for n in range(3):
-            pair_copy(s, n).wait_recv()
+        group(s, 10).wait_recv()
 
         def add(t, carry):
             parts[s][t, my_half] += cr[s, t]
@@ -406,58 +433,47 @@
         scatter_copy(q, 5).start()
 
     def step_first(q):
-        for n in range(2, 6):
-            scatter_copy(q, n).wait_recv()
-        bz[q] = parts[q // 2][:, chunk(q, 0)] + (rl[q] + rr[q])
+        group(q, 2).wait_recv()
+        bz[q] = parts[q // 2][:, chunk(q, 0)] + (lr[q, 0] + lr[q, 1])
         for off in FAR_FIRST:
             second_copy(q, off).start()
 
     def step_second(q):
-        for off in OFFS:
-            second_copy(q, off).wait_recv()
+        group(q, 3).wait_recv()
         c = coord[axes[q % 2][1]]
         xb[q, x] = (bz[q, pl.ds(c * TQ, TQ)] + r2[q, 0]) + (r2[q, 1] + r2[q, 2])
         for off in FAR_FIRST:
             third_copy(q, off, x).start()
 
     def step_third(q):
-        for off in OFFS:
-            third_copy(q, off, turn(x, RING - off)).wait_recv()
+        group(q, 4).wait_recv()
         c = coord[axes[q % 2][1]]
         ds[q, pl.ds(c * TQ, TQ)] = (xb[q, 0] + xb[q, 1]) + (xb[q, 2] + xb[q, 3])
         for off in FAR_FIRST:
             fourth_copy(q, off, c).start()
 
     def step_fourth(q):
-        c = coord[axes[q % 2][1]]
-        for off in OFFS:
-            fourth_copy(q, off, turn(c, RING - off)).wait_recv()
+        group(q, 5).wait_recv()
         for n in range(4):
             gather_copy(q, n).start()
-        out_copy(q, 0).start()
+        out_copy(q, 6).start()
         outs[q // 2][:, chunk(q, 0)] = ds[q, pl.ds(0, 27)]
 
     def step_forward(q):
-        gather_copy(q, 0).wait_recv()
-        gather_copy(q, 4).start()
-        gather_copy(q, 1).wait_recv()
-        gather_copy(q, 5).start()
+        for n in range(2):
+            gather_copy(q, n).wait_recv()
+            gather_copy(q, 4 + n).start()
+            out_copy(q, n).start()
 
     def step_fifth(q):
+        group(q, 8).wait_recv()
         for n in range(2, 6):
-            gather_copy(q, n).wait_recv()
-            out_copy(q, n - 1).start()
+            out_copy(q, n).start()
 
     def finish_sum(q):
-        for n in range(5):
-            out_copy(q, n).wait()
-        for n in range(6):
-            scatter_copy(q, n).wait_send()
-            gather_copy(q, n).wait_send()
-        for off in OFFS:
-            second_copy(q, off).wait_send()
-            third_copy(q, off, x).wait_send()
-            fourth_copy(q, off, coord[axes[q % 2][1]]).wait_send()
+        group(q, 9).wait_recv()
+        for n in range(10 if q > 1 else 11):
+            group(q, n).wait_send()
 
     def after_dw2(k):
         if k == 2:
@@ -469,8 +485,14 @@
     def after_dw1(k):
         if k >= 2:
             pair_copy(1, k - 2).start()
-        if k == 2:
-            both(step_relay, 0)
+
+    def finish_halos():
+        for k in range(4):
+            finish_halo(k)
+
+    def finish_sums():
+        for q in range(4):
+            finish_sum(q)
 
     loads[0].wait()
     loads[1].wait()
@@ -482,10 +504,9 @@
     conv_inner(ge, w2, acc2, True)
     pass_corners(0)
     take_faces(0)
-    conv_outer(xe, w1, acc1, False)
-    each_row(acc1, after_conv1)
+    conv_outer_rows(xe, w1, acc1, False, after_conv1)
     side(2).start()
-    each_face(2, start, range(NH))
+    each_face(2, start, every, every)
     pass_corners(1)
     side(2).wait_recv()
     conv_inner(ze, w2, acc1, False)
@@ -493,60 +514,56 @@
     take_faces(1)
     weight_grad(zt, ge, p2, True, (0, 2, 3), after_dw2)
     relay_far(2, hops[2])
-    conv_outer(ge, w2, acc2, True)
+    conv_outer_rows(ge, w2, acc2, True, after_conv_g)
     step_pair(0)
-    each_row(acc2, after_conv_g)
     side(3).start()
-    each_face(3, start, range(2))
+    each_face(3, start, early, early)
     weight_grad(at, xe, p1, False, range(5), after_dw1)
     pass_corners(2)
+    both(step_relay, dw2_q)
     step_pair(1)
     relay_far(3, (1,))
-    both(step_first, 0)
+    side(3).wait_recv()
+    conv_inner(ae, w1, acc2, True, 0, 1)
+    both(step_first, dw2_q)
+    both(step_relay, dw1_q)
     take_faces(2)
     conv_outer(ze, w2, acc1, False)
-    both(step_relay, 2)
-    side(3).wait_recv()
-    conv_inner(ae, w1, acc2, True, 0, 1)
-    both(step_second, 0)
-    each_face(3, start, (2, 3))
+    both(step_second, dw2_q)
+    each_face(3, start, late, late)
+    both(step_first, dw1_q)
     each_row(acc1, after_add(xe, y_out))
-    both(step_first, 2)
-    both(step_third, 0)
+    both(step_third, dw2_q)
     pass_corners(3)
+    both(step_second, dw1_q)
     conv_inner(ae, w1, acc2, True, 1, 2)
-    both(step_second, 2)
     relay_far(3, (3,))
-    both(step_fourth, 0)
-    both(step_third, 2)
-    both(step_forward, 0)
-    both(step_fourth, 2)
+    both(step_fourth, dw2_q)
+    both(step_third, dw1_q)
+    both(step_forward, dw2_q)
+    both(step_fourth, dw1_q)
     take_faces(3)
     conv_outer(ae, w1, acc2, True)
     each_row(acc2, after_add(ge, dx_out))
-    both(step_forward, 2)
-    both(step_fifth, 0)
-    both(step_fifth, 2)
-    for k in range(4):
-        finish_halo(k)
-    for q in range(4):
-        finish_sum(q)
-    for s in range(2):
-        for n in range(3):
-            pair_copy(s, n).wait_send()
+    both(step_forward, dw1_q)
+    both(step_fifth, dw2_q)
+    both(step_fifth, dw1_q)
+    finish_halos()
+    finish_sums()
 
 
 def to_hbm(y_vm, dx_vm, dw1_vm, dw2_vm, y_hbm, dx_hbm, dw1_hbm, dw2_hbm, sem):
-    copies = [(y_vm, y_hbm), (dx_vm, dx_hbm)]
-    for src, dst in ((dw1_vm, dw1_hbm), (dw2_vm, dw2_hbm)):
-        for td in range(3):
-            copies.append((src.at[pl.ds(td * 6, 6)], dst.at[pl.ds(td * 9, 6)]))
-            copies.append((src.at[pl.ds(TAIL + 3 * TAIL_ORDER.index(td), 3)], dst.at[pl.ds(td * 9 + 6, 3)]))
-    started = [pltpu.make_async_copy(src, dst, sem.at[n]) for n, (src, dst) in enumerate(copies)]
-    for copy in started:
-        copy.start()
-    for copy in started:
-        copy.wait()
+    pairs = ((y_vm, y_hbm), (dx_vm, dx_hbm), (dw1_vm, dw1_hbm), (dw2_vm, dw2_hbm))
+    for n, (src, dst) in enumerate(pairs):
+        if n < 2:
+            pltpu.make_async_copy(src, dst, sem.at[n]).start()
+        else:
+            for td in range(3):
+                pltpu.make_async_copy(src.at[pl.ds(td * 6, 6)], dst.at[pl.ds(td * 9, 6)], sem.at[n]).start()
+                tail = TAIL + 3 * TAIL_ORDER.index(td)
+                pltpu.make_async_copy(src.at[pl.ds(tail, 3)], dst.at[pl.ds(td * 9 + 6, 3)], sem.at[n]).start()
+    for n, (src, dst) in enumerate(pairs):
+        pltpu.make_async_copy(src, dst, sem.at[n]).wait()
 
 
 def solution(mesh):
@@ -579,19 +596,18 @@
                 pltpu.VMEM((2, TAPS, NC // 2, NC), F32),
                 pltpu.VMEM((4, TAPS // 2, NC // 16, NC), F32),
                 pltpu.VMEM((4, TAPS // 2, NC // 16, NC), F32),
-                pltpu.VMEM((4, TAPS, NC // 16, NC), F32),
-                pltpu.VMEM((4, TAPS, NC // 16, NC), F32),
+                pltpu.VMEM((4, 2, TAPS, NC // 16, NC), F32),
                 pltpu.VMEM((4, TAPS, NC // 16, NC), F32),
                 pltpu.VMEM((4, RING - 1, TQ, NC // 16, NC), F32),
                 pltpu.VMEM((4, RING, TQ, NC // 16, NC), F32),
                 pltpu.VMEM((4, TAPS, NC // 16, NC), F32),
                 pltpu.VMEM((2, 2, NB, 1, width, NC), BF16),
-                pltpu.SemaphoreType.DMA((4, 8)),
-                pltpu.SemaphoreType.DMA((4, 8)),
+                pltpu.SemaphoreType.DMA((4, 2)),
+                pltpu.SemaphoreType.DMA((4, 2, 2)),
                 pltpu.SemaphoreType.DMA((4, 3)),
                 pltpu.SemaphoreType.DMA((4, 3)),
-                pltpu.SemaphoreType.DMA((4, 29)),
-                pltpu.SemaphoreType.DMA((4, 29)),
+                pltpu.SemaphoreType.DMA((4, 11)),
+                pltpu.SemaphoreType.DMA((4, 11)),
                 pltpu.SemaphoreType.DMA((2, 4)),
                 pltpu.SemaphoreType.DMA((2, 2)),
                 pltpu.SemaphoreType.DMA((4,)),
@@ -608,7 +624,7 @@
             ),
             in_specs=[pl.BlockSpec(memory_space=pltpu.VMEM)] * 4,
             out_specs=(anywhere,) * 4,
-            scratch_shapes=[pltpu.SemaphoreType.DMA((14,))],
+            scratch_shapes=[pltpu.SemaphoreType.DMA((4,))],
             compiler_params=pltpu.CompilerParams(vmem_limit_bytes=4 * 1000 * 1000),
         )(*outs)
         shape = w_conv1.shape

time: 87.5 us -> 83.5 us (0.954)
  Pallas kernels: 86.6 us -> 82.6 us
    pallas_call x1, Pallas kernels: 84 us -> 80.1 us  [local_step(): pl.pallas_call(functools.partial(kernel, width, depth_count), out_shape=(...]
where the time goes in v4:
time: 83.5 us; the launch traced here: 83.4 us
  Pallas kernels  82.6 us (99%)
    pallas_call x1, Pallas kernels, local_step(): pl.pallas_call(functools.partial(kernel, width, depth_count), out_shape=(...  80.1 us
    pallas_call x1, Pallas kernels, local_step(): pl.pallas_call(to_hbm, out_shape=(jax.ShapeDtypeStruct(x_tile.shape, BF16...  2.47 us

profile of v4, /device:TPU:1, one launch (start us, length us, event | category | flops | bytes accessed | tf_op | source)
XLA Modules:
  0.0 83.4 jit_solution(17793086866992338575)
XLA Ops:
  0.6 80.1 %shard_map.75 = (bf16[2,2,4,256,128]{4,3,2,1,0:T(8,128)(2,1)S(1)}, bf16[2,2,4,256,128]{4,3,2,1,0:T(8,128)(2,1)S(1)}, f32[27,128,128]{2,1,0:T(8,128)S(1)}, f32[27,128,128]{2,1,0:T(8,128)S(1)}) custom-call(bf16[2,2,4,256,128]{4,3,2,1,0:T(8,128)(2,1)} %x_hbm.1, bf16[3,3,3,128,128]{4,3,2,1,0:T(8,128)(2,1)} %w1_hbm.1, bf16[3,3,3,128,128]{4,3,2,1,0:T(8,128)(2,1)} %w2_hbm.1, ...), custom_call_target="tpu_custom_call" | custom-call | tf_op jit(solution)/shard_map/pallas_call | solution.py:581
  80.8 2.5 %shard_map.76 = (bf16[2,2,4,256,128]{4,3,2,1,0:T(8,128)(2,1)}, bf16[2,2,4,256,128]{4,3,2,1,0:T(8,128)(2,1)}, f32[27,128,128]{2,1,0:T(8,128)}, f32[27,128,128]{2,1,0:T(8,128)}) custom-call(bf16[2,2,4,256,128]{4,3,2,1,0:T(8,128)(2,1)S(1)} %get-tuple-element.12.y_vm, bf16[2,2,4,256,128]{4,3,2,1,0:T(8,128)(2,1)S(1)} %get-tuple-element.13.dx_vm, ...), custom_call_target="tpu_custom_call" | custom-call | tf_op jit(solution)/shard_map/pallas_call | solution.py:617

commit v5 on v4

--- a/solution.py
+++ b/solution.py
@@ -301,31 +301,37 @@
     def tap_index(td, th):
         return td * 6 + th * 3 if th < 2 else TAIL + 3 * TAIL_ORDER.index(td)
 
-    def weight_grad(own_t, ext, part, swap, which, between):
-        def rhs(td, th):
-            d0, h0 = (2 - td, 2 - th) if swap else (td, th)
-            return jnp.concatenate([lines(ext, b, d + d0, h0) for b in range(NB) for d in range(ND)], axis=0)
-
-        def product(right):
+    def weight_grad(own_t, ext, part, swap, groups, between):
+        for k, (layers, taps, more) in enumerate(groups):
+            blocks = [(b, d) for b in range(NB) for d in layers]
+
+            def rhs(td, th):
+                d0, h0 = (2 - td, 2 - th) if swap else (td, th)
+                return jnp.concatenate([lines(ext, b, d + d0, h0) for b, d in blocks], axis=0)
+
+            right = jnp.concatenate([rhs(*t) for t in taps], axis=1)
             cut = 3 * NC // 2
             halves = []
             for top in (0, cut):
-                lhs = jnp.concatenate([own_t[i, pl.ds(top, cut)] for i in range(NB * ND * NH)], axis=1)
+                lhs = jnp.concatenate([own_t[(b * ND + d) * NH + h, pl.ds(top, cut)] for b, d in blocks for h in range(NH)], axis=1)
                 halves.append(jnp.dot(lhs, right, preferred_element_type=F32))
-            return jnp.concatenate(halves, axis=0)
-
-        def put(out, n, td, th):
-            for tw in range(3):
-                blk = out[tw * NC:(tw + 1) * NC, n * NC:(n + 1) * NC]
-                part[tap_index(td, th) + tw] = blk if swap else blk.T
-
-        groups = [((td, 0), (td, 1)) for td in range(3)] + [((0, 2), (2, 2)), ((1, 2),)]
-        for k in which:
-            taps = groups[k]
-            out = product(jnp.concatenate([rhs(*t) for t in taps], axis=1))
-            for n, t in enumerate(taps):
-                put(out, n, *t)
+            out = jnp.concatenate(halves, axis=0)
+            for n, (td, th) in enumerate(taps):
+                for tw in range(3):
+                    blk = out[tw * NC:(tw + 1) * NC, n * NC:(n + 1) * NC]
+                    to = tap_index(td, th) + tw
+                    blk = blk if swap else blk.T
+                    part[to] = part[to] + blk if more else blk
             between(k)
+
+    both_layers = tuple(range(ND))
+    dw1_groups = [(both_layers, ((td, 0), (td, 1)), False) for td in range(3)] + [(both_layers, ((0, 2), (2, 2)), False), (both_layers, ((1, 2),), False)]
+
+    def plane(td):
+        return tuple((td, th) for th in range(3))
+
+    dw2_inner = [dw1_groups[1], dw1_groups[4], ((0,), plane(0), False), ((1,), plane(2), False)]
+    dw2_outer = [((1,), plane(0), True), ((0,), plane(2), True)]
 
     half, piece = NC // 2, NC // 16
     axes = (("y", "z"), ("z", "y"))
@@ -336,7 +342,7 @@
     high27 = pl.ds(TAPS // 2, TAPS // 2 - 1)
 
     def sems(q, n):
-        return ar_send.at[q, n], ar_recv.at[q, n]
+        return ar_send.at[q, n // 10], ar_recv.at[q, n]
 
     def turn(c, off):
         return lax.rem(c + off, RING)
@@ -395,11 +401,9 @@
         return rdma(src, out.at[taps, chunk(q, off)], *sems(q, 9), (other, dep))
 
     def group(q, n):
-        ref = {
-            0: ra.at[q], 1: rb.at[q], 2: lr.at[q], 3: r2.at[q], 4: r2.at[q], 5: r2.at[q],
-            6: ra.at[q], 7: ra.at[q, pl.ds(1, TAPS // 2 - 1)],
-            8: outs[0].at[:, pl.ds(0, 2 * piece)], 9: outs[0].at[:, pl.ds(0, 4 * piece)], 10: cr.at[0],
-        }[n]
+        bands = [outs[0].at[:, pl.ds(0, k * piece)] for k in (2, 4)]
+        refs = [ra.at[q], rb.at[q], lr.at[q]] + [r2.at[q]] * 3 + [ra.at[q], ra.at[q, pl.ds(1, TAPS // 2 - 1)]] + bands + [cr.at[0]]
+        ref = refs[n]
         return rdma(ref, ref, *sems(q, n), (other, dep))
 
     my_half = pl.ds(pl.multiple_of(row * half, half), half)
@@ -472,15 +476,15 @@
 
     def finish_sum(q):
         group(q, 9).wait_recv()
-        for n in range(10 if q > 1 else 11):
-            group(q, n).wait_send()
+        all_sent = cr.at[:, :, pl.ds(0, 6 * piece)]
+        rdma(all_sent, all_sent, *sems(q, 0), (other, dep)).wait_send()
+        if q < 2:
+            group(q, 10).wait_send()
 
     def after_dw2(k):
-        if k == 2:
-            pair_copy(0, 0).start()
-        if k == 3:
-            pair_copy(0, 1).start()
-            pair_copy(0, 2).start()
+        if k == 1:
+            for n in range(3):
+                pair_copy(0, n).start()
 
     def after_dw1(k):
         if k >= 2:
@@ -510,28 +514,29 @@
     pass_corners(1)
     side(2).wait_recv()
     conv_inner(ze, w2, acc1, False)
-    weight_grad(zt, ge, p2, True, (1, 4), after_dw2)
+    weight_grad(zt, ge, p2, True, dw2_inner, lambda k: None)
     take_faces(1)
-    weight_grad(zt, ge, p2, True, (0, 2, 3), after_dw2)
+    weight_grad(zt, ge, p2, True, dw2_outer, after_dw2)
     relay_far(2, hops[2])
     conv_outer_rows(ge, w2, acc2, True, after_conv_g)
     step_pair(0)
     side(3).start()
     each_face(3, start, early, early)
-    weight_grad(at, xe, p1, False, range(5), after_dw1)
+    weight_grad(at, xe, p1, False, dw1_groups, after_dw1)
     pass_corners(2)
     both(step_relay, dw2_q)
     step_pair(1)
-    relay_far(3, (1,))
     side(3).wait_recv()
     conv_inner(ae, w1, acc2, True, 0, 1)
+    relay_far(3, (1,))
     both(step_first, dw2_q)
     both(step_relay, dw1_q)
     take_faces(2)
     conv_outer(ze, w2, acc1, False)
     both(step_second, dw2_q)
-    each_face(3, start, late, late)
+    each_face(3, start, late, ())
     both(step_first, dw1_q)
+    each_face(3, start, (), late)
     each_row(acc1, after_add(xe, y_out))
     both(step_third, dw2_q)
     pass_corners(3)
@@ -606,7 +611,7 @@
                 pltpu.SemaphoreType.DMA((4, 2, 2)),
                 pltpu.SemaphoreType.DMA((4, 3)),
                 pltpu.SemaphoreType.DMA((4, 3)),
-                pltpu.SemaphoreType.DMA((4, 11)),
+                pltpu.SemaphoreType.DMA((4, 2)),
                 pltpu.SemaphoreType.DMA((4, 11)),
                 pltpu.SemaphoreType.DMA((2, 4)),
                 pltpu.SemaphoreType.DMA((2, 2)),

time: 83.5 us -> 82.5 us (0.988)
  Pallas kernels: 82.6 us -> 81.5 us
    pallas_call x1, Pallas kernels: 80.1 us -> 79.1 us  [local_step(): pl.pallas_call(functools.partial(kernel, width, depth_count), out_shape=(...]
where the time goes in v5:
time: 82.5 us; the launch traced here: 82.3 us
  Pallas kernels  81.5 us (99%)
    pallas_call x1, Pallas kernels, local_step(): pl.pallas_call(functools.partial(kernel, width, depth_count), out_shape=(...  79.1 us
    pallas_call x1, Pallas kernels, local_step(): pl.pallas_call(to_hbm, out_shape=(jax.ShapeDtypeStruct(x_tile.shape, BF16...  2.47 us

profile of v5, /device:TPU:1, one launch (start us, length us, event | category | flops | bytes accessed | tf_op | source)
XLA Modules:
  0.0 82.3 jit_solution(13840847563070055616)
XLA Ops:
  0.6 79.1 %shard_map.75 = (bf16[2,2,4,256,128]{4,3,2,1,0:T(8,128)(2,1)S(1)}, bf16[2,2,4,256,128]{4,3,2,1,0:T(8,128)(2,1)S(1)}, f32[27,128,128]{2,1,0:T(8,128)S(1)}, f32[27,128,128]{2,1,0:T(8,128)S(1)}) custom-call(bf16[2,2,4,256,128]{4,3,2,1,0:T(8,128)(2,1)} %x_hbm.1, bf16[3,3,3,128,128]{4,3,2,1,0:T(8,128)(2,1)} %w1_hbm.1, bf16[3,3,3,128,128]{4,3,2,1,0:T(8,128)(2,1)} %w2_hbm.1, ...), custom_call_target="tpu_custom_call" | custom-call | tf_op jit(solution)/shard_map/pallas_call | solution.py:586
  79.7 2.5 %shard_map.76 = (bf16[2,2,4,256,128]{4,3,2,1,0:T(8,128)(2,1)}, bf16[2,2,4,256,128]{4,3,2,1,0:T(8,128)(2,1)}, f32[27,128,128]{2,1,0:T(8,128)}, f32[27,128,128]{2,1,0:T(8,128)}) custom-call(bf16[2,2,4,256,128]{4,3,2,1,0:T(8,128)(2,1)S(1)} %get-tuple-element.12.y_vm, bf16[2,2,4,256,128]{4,3,2,1,0:T(8,128)(2,1)S(1)} %get-tuple-element.13.dx_vm, ...), custom_call_target="tpu_custom_call" | custom-call | tf_op jit(solution)/shard_map/pallas_call | solution.py:622

commit v6 on v5

--- a/solution.py
+++ b/solution.py
@@ -342,7 +342,7 @@
     high27 = pl.ds(TAPS // 2, TAPS // 2 - 1)
 
     def sems(q, n):
-        return ar_send.at[q, n // 10], ar_recv.at[q, n]
+        return ar_send.at[q, n // 11], ar_recv.at[q, n]
 
     def turn(c, off):
         return lax.rem(c + off, RING)
@@ -354,7 +354,7 @@
     def pair_copy(s, n):
         theirs = pl.ds(pl.multiple_of(other * half, half), half)
         taps = (pl.ds(0, TAIL), pl.ds(TAIL, 6), pl.ds(TAIL + 6, 4))[n]
-        return rdma(parts[s].at[taps, theirs], cr.at[s, taps], *sems(s, 10), (other, dep))
+        return rdma(parts[s].at[taps, theirs], cr.at[s, taps], *sems(s, 11), (other, dep))
 
     def scatter_copy(q, n):
         part = parts[q // 2]
@@ -392,16 +392,16 @@
             (high27, 1, prv),
         )[n]
         src = ds.at[q, taps] if n < 4 else out.at[taps, chunk(q, off)]
-        return rdma(src, out.at[taps, chunk(q, off)], *sems(q, 6 + min(n, 2)), dev)
+        return rdma(src, out.at[taps, chunk(q, off)], *sems(q, 6 + min(n, 2) + n // 4), dev)
 
     def out_copy(q, n):
         out = outs[q // 2]
         taps, off = ((low, 3), (high27, 1), (high27, 3), (low, 1), (low, 2), (high27, 2), (pl.ds(0, 27), 0))[n]
         src = ds.at[q, taps] if off == 0 else out.at[taps, chunk(q, off)]
-        return rdma(src, out.at[taps, chunk(q, off)], *sems(q, 9), (other, dep))
+        return rdma(src, out.at[taps, chunk(q, off)], *sems(q, 10), (other, dep))
 
     def group(q, n):
-        bands = [outs[0].at[:, pl.ds(0, k * piece)] for k in (2, 4)]
+        bands = [outs[0].at[:, pl.ds(0, k * piece)] for k in (1, 1, 4)]
         refs = [ra.at[q], rb.at[q], lr.at[q]] + [r2.at[q]] * 3 + [ra.at[q], ra.at[q, pl.ds(1, TAPS // 2 - 1)]] + bands + [cr.at[0]]
         ref = refs[n]
         return rdma(ref, ref, *sems(q, n), (other, dep))
@@ -415,7 +415,7 @@
         step(q + 1)
 
     def step_pair(s):
-        group(s, 10).wait_recv()
+        group(s, 11).wait_recv()
 
         def add(t, carry):
             parts[s][t, my_half] += cr[s, t]
@@ -470,16 +470,17 @@
             out_copy(q, n).start()
 
     def step_fifth(q):
-        group(q, 8).wait_recv()
-        for n in range(2, 6):
-            out_copy(q, n).start()
+        for n in (8, 9):
+            group(q, n).wait_recv()
+            for piece_n in (2 * n - 14, 2 * n - 13):
+                out_copy(q, piece_n).start()
 
     def finish_sum(q):
-        group(q, 9).wait_recv()
+        group(q, 10).wait_recv()
         all_sent = cr.at[:, :, pl.ds(0, 6 * piece)]
         rdma(all_sent, all_sent, *sems(q, 0), (other, dep)).wait_send()
         if q < 2:
-            group(q, 10).wait_send()
+            group(q, 11).wait_send()
 
     def after_dw2(k):
         if k == 1:
@@ -612,7 +613,7 @@
                 pltpu.SemaphoreType.DMA((4, 3)),
                 pltpu.SemaphoreType.DMA((4, 3)),
                 pltpu.SemaphoreType.DMA((4, 2)),
-                pltpu.SemaphoreType.DMA((4, 11)),
+                pltpu.SemaphoreType.DMA((4, 12)),
                 pltpu.SemaphoreType.DMA((2, 4)),
                 pltpu.SemaphoreType.DMA((2, 2)),
                 pltpu.SemaphoreType.DMA((4,)),

time: 82.5 us -> 82.3 us (level)
  no operation moved by 1% of the time
where the time goes in v6:
time: 82.3 us; the launch traced here: 82.2 us
  Pallas kernels  81.4 us (99%)
    pallas_call x1, Pallas kernels, local_step(): pl.pallas_call(functools.partial(kernel, width, depth_count), out_shape=(...  78.9 us
    pallas_call x1, Pallas kernels, local_step(): pl.pallas_call(to_hbm, out_shape=(jax.ShapeDtypeStruct(x_tile.shape, BF16...  2.47 us

profile of v6, /device:TPU:1, one launch (start us, length us, event | category | flops | bytes accessed | tf_op | source)
XLA Modules:
  0.0 82.2 jit_solution(8556619084339397017)
XLA Ops:
  0.6 78.9 %shard_map.75 = (bf16[2,2,4,256,128]{4,3,2,1,0:T(8,128)(2,1)S(1)}, bf16[2,2,4,256,128]{4,3,2,1,0:T(8,128)(2,1)S(1)}, f32[27,128,128]{2,1,0:T(8,128)S(1)}, f32[27,128,128]{2,1,0:T(8,128)S(1)}) custom-call(bf16[2,2,4,256,128]{4,3,2,1,0:T(8,128)(2,1)} %x_hbm.1, bf16[3,3,3,128,128]{4,3,2,1,0:T(8,128)(2,1)} %w1_hbm.1, bf16[3,3,3,128,128]{4,3,2,1,0:T(8,128)(2,1)} %w2_hbm.1, ...), custom_call_target="tpu_custom_call" | custom-call | tf_op jit(solution)/shard_map/pallas_call | solution.py:587
  79.6 2.5 %shard_map.76 = (bf16[2,2,4,256,128]{4,3,2,1,0:T(8,128)(2,1)}, bf16[2,2,4,256,128]{4,3,2,1,0:T(8,128)(2,1)}, f32[27,128,128]{2,1,0:T(8,128)}, f32[27,128,128]{2,1,0:T(8,128)}) custom-call(bf16[2,2,4,256,128]{4,3,2,1,0:T(8,128)(2,1)S(1)} %get-tuple-element.12.y_vm, bf16[2,2,4,256,128]{4,3,2,1,0:T(8,128)(2,1)S(1)} %get-tuple-element.13.dx_vm, ...), custom_call_target="tpu_custom_call" | custom-call | tf_op jit(solution)/shard_map/pallas_call | solution.py:623

commit v7 on v6

--- a/solution.py
+++ b/solution.py
@@ -549,8 +549,7 @@
     both(step_forward, dw2_q)
     both(step_fourth, dw1_q)
     take_faces(3)
-    conv_outer(ae, w1, acc2, True)
-    each_row(acc2, after_add(ge, dx_out))
+    conv_outer_rows(ae, w1, acc2, True, after_add(ge, dx_out))
     both(step_forward, dw1_q)
     both(step_fifth, dw2_q)
     both(step_fifth, dw1_q)

time: 82.3 us -> 82.4 us (level)
  no operation moved by 1% of the time
where the time goes in v7:
time: 82.4 us; the launch traced here: 82.3 us
  Pallas kernels  81.5 us (99%)
    pallas_call x1, Pallas kernels, local_step(): pl.pallas_call(functools.partial(kernel, width, depth_count), out_shape=(...  79 us
    pallas_call x1, Pallas kernels, local_step(): pl.pallas_call(to_hbm, out_shape=(jax.ShapeDtypeStruct(x_tile.shape, BF16...  2.47 us

profile of v7, /device:TPU:1, one launch (start us, length us, event | category | flops | bytes accessed | tf_op | source)
XLA Modules:
  0.0 82.3 jit_solution(12066300332290391853)
XLA Ops:
  0.6 79.0 %shard_map.75 = (bf16[2,2,4,256,128]{4,3,2,1,0:T(8,128)(2,1)S(1)}, bf16[2,2,4,256,128]{4,3,2,1,0:T(8,128)(2,1)S(1)}, f32[27,128,128]{2,1,0:T(8,128)S(1)}, f32[27,128,128]{2,1,0:T(8,128)S(1)}) custom-call(bf16[2,2,4,256,128]{4,3,2,1,0:T(8,128)(2,1)} %x_hbm.1, bf16[3,3,3,128,128]{4,3,2,1,0:T(8,128)(2,1)} %w1_hbm.1, bf16[3,3,3,128,128]{4,3,2,1,0:T(8,128)(2,1)} %w2_hbm.1, ...), custom_call_target="tpu_custom_call" | custom-call | tf_op jit(solution)/shard_map/pallas_call | solution.py:586
  79.6 2.5 %shard_map.76 = (bf16[2,2,4,256,128]{4,3,2,1,0:T(8,128)(2,1)}, bf16[2,2,4,256,128]{4,3,2,1,0:T(8,128)(2,1)}, f32[27,128,128]{2,1,0:T(8,128)}, f32[27,128,128]{2,1,0:T(8,128)}) custom-call(bf16[2,2,4,256,128]{4,3,2,1,0:T(8,128)(2,1)S(1)} %get-tuple-element.12.y_vm, bf16[2,2,4,256,128]{4,3,2,1,0:T(8,128)(2,1)S(1)} %get-tuple-element.13.dx_vm, ...), custom_call_target="tpu_custom_call" | custom-call | tf_op jit(solution)/shard_map/pallas_call | solution.py:622
